TPU v7x, 1024 devices: a whole 4x4x32 slice. The times are simulated.
1024 devices in a mesh: prompt: 64 (over z, core), sample: 4 (over x), vocab: 4 (over y).
Axes of the slice: x: 4, y: 4, z: 32, core: 2. Of those that a mesh axis runs over, the one named last changes fastest.
Arguments:
- hidden: bfloat16 [4, 768, 3584], P('sample', ('prompt', 'vocab')), may hold values from -170 to 170
- unembed: bfloat16 [152064, 3584], P(('prompt', 'vocab')), may hold values from -1 to 1
- token_ids: int32 [4, 768], P('sample', ('prompt', 'vocab')), may hold values from 0 to 152063, as said below
- old_logp: float32 [4, 768], P('sample', ('prompt', 'vocab')), may hold values from -14 to -11
- ref_logp: float32 [4, 768], P('sample', ('prompt', 'vocab')), may hold values from -14 to -11
- loss_mask: int32 [4, 768], P('sample', ('prompt', 'vocab')), may hold values 0 or 1
- lengths: int32 [64, 4], P('prompt', 'sample'), may hold values from 1 to 12, as said below
- sample_valid: int32 [64, 4], P('prompt', 'sample'), may hold values 0 or 1
- rewards: int32 [64, 4], P('prompt', 'sample'), may hold values from -300 to 300
Outputs:
- token_logp: float32 [4, 768], P('sample', ('prompt', 'vocab'))
- token_loss: float32 [4, 768], P('sample', ('prompt', 'vocab'))
- advantages: float32 [64, 4], P('prompt', 'sample')
- loss: float32 [], replicated
Inputs may be any that keep to these rules, and one draw needn't show every extreme that they name: `token_ids`: token ids name vocabulary entries. `lengths`: some response in every draw has length 12.
All inputs are finite; a program needn't handle non-finite values. No bound on the sum of `loss_mask` or of `sample_valid` on one device may be relied on, other than what follows from the above.
Results may differ from a plain program's by a relative error of at most 0.0003.
Values may be sent and summed in bfloat16 or wider, within the bound.
No kernel may reach another device: no remote copies, remote signals or barrier semaphores. Data moves between devices by JAX's collectives and lax.ppermute only.
A program may use at most 64 MiB of HBM per device.

v0:
```python
import math

import jax
import jax.numpy as jnp
from jax import lax
from jax.sharding import Mesh
from jax.sharding import PartitionSpec as P

PROMPT_VOCAB = ("prompt_0", "prompt_1", "vocab")
PROMPT_SAMPLE_VOCAB = ("prompt_0", "prompt_1", "sample", "vocab")
PROMPT = ("prompt_0", "prompt_1")


clip_low = 0.8
clip_high = 1.2
dual_clip = 3.0
kl_weight = 0.04
reward_unit = 0.01
std_floor = 0.5


def from_everyone(array, axis):
    devices = lax.axis_size(axis)
    return lax.all_to_all(
        jnp.broadcast_to(array[None], (devices, *array.shape)), axis, 0, 0, tiled=True
    )


def over_copies(array, axis):
    everything = from_everyone(array, axis)
    return jnp.sum(everything, axis=0)


def together(arrays, axis):
    ends = [0]
    for a in arrays:
        ends.append(ends[-1] + a.size)
    total = over_copies(jnp.concatenate([a.ravel() for a in arrays]), axis)
    return tuple((total[b:e].reshape(a.shape) for a, b, e in zip(arrays, ends, ends[1:])))


def sent_together(arrays, axis, dim, along):
    both = jnp.concatenate(arrays, axis=along)
    out, at, gathered = (lax.all_gather(both, axis, axis=dim, tiled=True), 0, [])
    for a in arrays:
        gathered.append(lax.slice_in_dim(out, at, at + a.shape[along], axis=along))
        at += a.shape[along]
    return tuple(gathered)


def over_axes(array, axes):
    for axis in axes:
        array = lax.pmax(array, axis)
    return array


def by_axis(array, axes):
    for axis in axes:
        array = lax.psum(array, axis)
    return array


def shard_stats(row_block, labels, weight, vocab_start):
    logits = lax.dot_general(
        row_block, weight, (((1,), (1,)), ((), ())), preferred_element_type=jnp.float32
    )
    local_peak = jnp.max(logits, axis=1)
    exp_total = jnp.sum(jnp.exp(logits - local_peak[:, None]), axis=1)
    column = vocab_start + lax.broadcasted_iota(jnp.int32, logits.shape, 1)
    target = jnp.sum(jnp.where(column == labels[:, None], logits, 0.0), axis=1)
    return (local_peak, exp_total, target)


def local(
    hidden, unembed, token_ids, old_logp, ref_logp, loss_mask, lengths, sample_valid, rewards
):
    samples, local_rows, width = hidden.shape
    vocab_rows = unembed.shape[0]
    vocab_start = lax.axis_index(PROMPT_VOCAB) * vocab_rows
    gathered_rows = local_rows * lax.axis_size(PROMPT_VOCAB)
    flat_count = samples * gathered_rows
    positions = lax.axis_index("vocab") * local_rows + lax.broadcasted_iota(
        jnp.int32, (samples, local_rows), 1
    )
    live_rows = (loss_mask == 1) & (positions < lengths.T) & (sample_valid.T == 1)
    live_float = live_rows.astype(jnp.float32)
    valid_f = sample_valid.astype(jnp.float32)
    scores = rewards.astype(jnp.float32) * reward_unit
    group_count, first_moment, second_moment = together(
        (
            jnp.sum(valid_f, axis=1),
            jnp.sum(valid_f * scores, axis=1),
            jnp.sum(valid_f * scores * scores, axis=1),
        ),
        "sample",
    )
    safe_count = jnp.maximum(group_count, 1.0)
    group_mean = first_moment / safe_count
    spread = jnp.sqrt(jnp.maximum(second_moment / safe_count - group_mean * group_mean, 0.0))
    advantages = valid_f * (scores - group_mean[:, None]) / jnp.maximum(spread, std_floor)[:, None]
    whole_hidden, whole_ids, whole_live = (
        lax.all_gather(hidden, PROMPT_VOCAB, axis=1, tiled=True),
        *sent_together((token_ids, live_rows.astype(jnp.int32)), PROMPT_VOCAB, 1, 0),
    )
    rows_flat = whole_hidden.reshape(flat_count, width)
    ids_flat = whole_ids.reshape(flat_count)
    live_flat = whole_live.reshape(flat_count)
    row_order = jnp.argsort(1 - live_flat, stable=True)
    packed_rows = rows_flat[row_order]
    packed_ids = ids_flat[row_order]
    block_rows = math.gcd(flat_count, 128)
    live_used = jnp.sum(live_flat)
    turn_count = (live_used + block_rows - 1) // block_rows

    def one_block(turn_idx, totals):
        row_start = turn_idx * block_rows
        block_stats = shard_stats(
            lax.dynamic_slice_in_dim(packed_rows, row_start, block_rows, 0),
            lax.dynamic_slice_in_dim(packed_ids, row_start, block_rows, 0),
            unembed,
            vocab_start,
        )
        return (
            lax.dynamic_update_slice_in_dim(totals[0], block_stats[0], row_start, 0),
            lax.dynamic_update_slice_in_dim(totals[1], block_stats[1], row_start, 0),
            lax.dynamic_update_slice_in_dim(totals[2], block_stats[2], row_start, 0),
        )

    start_fill = (
        jnp.zeros((flat_count,), jnp.float32),
        jnp.ones((flat_count,), jnp.float32),
        jnp.zeros((flat_count,), jnp.float32),
    )
    packed_peak, packed_total, packed_target = lax.fori_loop(0, turn_count, one_block, start_fill)
    inverse = jnp.argsort(row_order)
    local_peak = packed_peak[inverse].reshape(samples, gathered_rows)
    exp_total = packed_total[inverse].reshape(samples, gathered_rows)
    target = packed_target[inverse].reshape(samples, gathered_rows)
    row_top = over_axes(local_peak, PROMPT_VOCAB)
    total_all, target_all = (
        by_axis(exp_total * jnp.exp(local_peak - row_top), PROMPT_VOCAB),
        by_axis(target, PROMPT_VOCAB),
    )
    own_start = lax.axis_index(PROMPT_VOCAB) * local_rows

    def own_rows(values):
        return lax.dynamic_slice_in_dim(values, own_start, local_rows, 1)

    raw_logp = own_rows(target_all) - (own_rows(row_top) + jnp.log(own_rows(total_all)))
    token_logp = jnp.where(live_rows, raw_logp, 0.0)
    adv_rows = advantages.T
    prob_ratio = jnp.exp(raw_logp - old_logp)
    gain_side = adv_rows * jnp.minimum(prob_ratio, clip_high)
    loss_side = jnp.maximum(adv_rows * jnp.maximum(prob_ratio, clip_low), dual_clip * adv_rows)
    objective = jnp.where(adv_rows >= 0.0, gain_side, loss_side)
    log_gap = ref_logp - raw_logp
    kl_term = jnp.exp(log_gap) - log_gap - 1.0
    token_loss = jnp.where(live_rows, kl_weight * kl_term - objective, 0.0)
    loss_part = jnp.sum(token_loss)
    loss_total, live_total = (
        by_axis(loss_part, PROMPT_SAMPLE_VOCAB),
        by_axis(jnp.sum(live_float), PROMPT_SAMPLE_VOCAB),
    )
    loss = loss_total / jnp.maximum(live_total, 1.0)
    return (token_logp, token_loss, advantages, loss)


def solution(mesh):
    split = Mesh(
        mesh.devices.reshape(32, 2, mesh.shape["sample"], mesh.shape["vocab"]),
        ("prompt_0", "prompt_1", "sample", "vocab"),
    )
    in_specs = (
        P("sample", PROMPT_VOCAB, None),
        P(PROMPT_VOCAB, None),
        P("sample", PROMPT_VOCAB),
        P("sample", PROMPT_VOCAB),
        P("sample", PROMPT_VOCAB),
        P("sample", PROMPT_VOCAB),
        P(PROMPT, "sample"),
        P(PROMPT, "sample"),
        P(PROMPT, "sample"),
    )
    out_specs = (P("sample", PROMPT_VOCAB), P("sample", PROMPT_VOCAB), P(PROMPT, "sample"), P())
    return jax.shard_map(local, mesh=split, in_specs=in_specs, out_specs=out_specs, check_vma=False)
```

profile of v0, /device:TPU:1, one launch (start us, length us, event | category | flops | bytes accessed | tf_op | source)
XLA Modules:
  0.0 602.7 jit_solution(4129452228153503567)
XLA Ops:
  7.2 1.4 copy.24
  10.5 4.8 all-to-all-start
  17.9 304.2 %all-gather = s32[256,3,2]{1,2,0:T(2,128)S(1)} all-gather(s32[1,3,2]{1,2,0:T(2,128)S(1)} %add_bitcast_fusion), channel_id=1, replica_groups=mesh['prompt_0'=32,'prompt_1'=2,'sample'=4,'vocab'=4] {'prompt_0','promp..., dimensions={0}, use_global_device_ids=true | all-gather | bytes 6168 | tf_op jit(solution)/shard_map/all_gather | solution.py:44
  323.7 4.4 sort.34
  328.0 4.4 sort.35
  332.4 3.2 gather_fusion.1
  338.3 7.8 %copy.32 = bf16[1,768,3584]{2,1,0:T(8,128)(2,1)} copy(bf16[1,768,3584]{2,0,1:T(2,128)(2,1)} %all-gather.3.cloned.1.call-done) | data formatting | bytes 11010048
  346.2 14.2 %gather_fusion = bf16[768,3584]{1,0:T(8,128)(2,1)} fusion(bf16[768,3584]{1,0:T(8,128)(2,1)} %bitcast.24, s32[1024]{0:T(1024)S(1)} %pad_clamp_fusion.1), kind=kCustom, calls=%fused_computation | custom fusion | bytes 11013120 | tf_op jit(solution)/shard_map/gather | solution.py:109
  360.4 4.7 while.14
  360.4 3.8 fusion.19
  365.1 3.2 gather_fusion.4
  368.3 3.2 gather_fusion.3
  371.5 42.4 %pmax.21 = f32[1,768]{1,0:T(1,128)S(1)} all-reduce(f32[1,768]{1,0:T(1,128)S(1)} %reshape.62), channel_id=1, replica_groups=mesh['prompt_0'=32,'prompt_1'=2,'sample'=4,'vocab'=4] {'prompt_0'}, use_global_device_ids=true, to_apply=%region_11.12 | all-reduce | flops 768 | bytes 6144 | tf_op jit(solution)/shard_map/pmax | solution.py:53
  414.0 13.1 %pmax.22 = f32[1,768]{1,0:T(1,128)S(1)} all-reduce(f32[1,768]{1,0:T(1,128)S(1)} %pmax.21), channel_id=1, replica_groups=mesh['prompt_0'=32,'prompt_1'=2,'sample'=4,'vocab'=4] {'prompt_1'}, use_global_device_ids=true, to_apply=%region_12.13 | all-reduce | flops 768 | bytes 6144 | tf_op jit(solution)/shard_map/pmax | solution.py:53
  427.1 7.7 %pmax.23 = f32[1,768]{1,0:T(1,128)S(1)} all-reduce(f32[1,768]{1,0:T(1,128)S(1)} %pmax.22), channel_id=1, replica_groups=mesh['prompt_0'=32,'prompt_1'=2,'sample'=4,'vocab'=4] {'vocab'}, use_global_device_ids=true, to_apply=%region_13.14 | all-reduce | flops 768 | bytes 6144 | tf_op jit(solution)/shard_map/pmax | solution.py:53
  434.8 3.2 gather_fusion.2
  438.0 42.9 %all-reduce.1 = (f32[1,768]{1,0:T(1,128)S(1)}, f32[1,768]{1,0:T(1,128)S(1)}) all-reduce(f32[1,768]{1,0:T(1,128)S(1)} %reshape.61, f32[1,768]{1,0:T(1,128)S(1)} %exponential_multiply_fusion), channel_id=1, replica_groups=mesh['prompt_0'=32,'prompt_1'=2,'sample'=4,'vocab'=4] {'prompt_0'}, use_global_device_ids=true, to_apply=%region_8.9 | all-reduce | flops 1536 | bytes 12288 | tf_op jit(solution)/shard_map/psum | solution.py:59
  480.9 18.6 %all-reduce.6 = (f32[1,768]{1,0:T(1,128)S(1)}, f32[1,768]{1,0:T(1,128)S(1)}) all-reduce(f32[1,768]{1,0:T(1,128)S(1)} %get-tuple-element.86, f32[1,768]{1,0:T(1,128)S(1)} %get-tuple-element.87), channel_id=1, replica_groups=mesh['prompt_0'=32,'prompt_1'=2,'sample'=4,'vocab'=4] {'prompt_1'}, use_global_device_ids=true, to_apply=%region_9.10 | all-reduce | flops 1536 | bytes 12288 | tf_op jit(solution)/shard_map/psum | solution.py:59
  499.5 6.1 %all-reduce.3 = (f32[1,768]{1,0:T(1,128)S(1)}, f32[1,768]{1,0:T(1,128)S(1)}) all-reduce(f32[1,768]{1,0:T(1,128)S(1)} %get-tuple-element.96, f32[1,768]{1,0:T(1,128)S(1)} %get-tuple-element.97), channel_id=1, replica_groups=mesh['prompt_0'=32,'prompt_1'=2,'sample'=4,'vocab'=4] {'vocab'}, use_global_device_ids=true, to_apply=%region_10.11 | all-reduce | flops 1536 | bytes 12288 | tf_op jit(solution)/shard_map/psum | solution.py:59
  505.6 1.3 fusion.10
  506.9 39.6 %all-reduce = (f32[]{:T(128)}, f32[]{:T(128)}) all-reduce(f32[]{:T(128)} %get-tuple-element.100, f32[]{:T(128)} %get-tuple-element.98), channel_id=1, replica_groups=mesh['prompt_0'=32,'prompt_1'=2,'sample'=4,'vocab'=4] {'prompt_0'}, use_global_device_ids=true, to_apply=%region_19.20 | all-reduce | flops 2 | bytes 16 | tf_op jit(solution)/shard_map/psum | solution.py:59
  546.5 18.5 %all-reduce.5 = (f32[]{:T(128)}, f32[]{:T(128)}) all-reduce(f32[]{:T(128)} %get-tuple-element.84, f32[]{:T(128)} %get-tuple-element.85), channel_id=1, replica_groups=mesh['prompt_0'=32,'prompt_1'=2,'sample'=4,'vocab'=4] {'prompt_1'}, use_global_device_ids=true, to_apply=%region_20.21 | all-reduce | flops 2 | bytes 16 | tf_op jit(solution)/shard_map/psum | solution.py:59
  565.0 18.4 %all-reduce.4 = (f32[]{:T(128)}, f32[]{:T(128)}) all-reduce(f32[]{:T(128)} %get-tuple-element.94, f32[]{:T(128)} %get-tuple-element.95), channel_id=1, replica_groups=mesh['prompt_0'=32,'prompt_1'=2,'sample'=4,'vocab'=4] {'sample'}, use_global_device_ids=true, to_apply=%region_21.22 | all-reduce | flops 2 | bytes 16 | tf_op jit(solution)/shard_map/psum | solution.py:59
  583.4 8.3 %all-reduce.2 = (f32[]{:T(128)}, f32[]{:T(128)}) all-reduce(f32[]{:T(128)} %get-tuple-element.92, f32[]{:T(128)} %get-tuple-element.93), channel_id=1, replica_groups=mesh['prompt_0'=32,'prompt_1'=2,'sample'=4,'vocab'=4] {'vocab'}, use_global_device_ids=true, to_apply=%region_22.23 | all-reduce | flops 2 | bytes 16 | tf_op jit(solution)/shard_map/psum | solution.py:59
  (37 shorter events, 5.6 us)
Async XLA Ops:
  7.2 331.2 %all-gather.3.cloned.1.call-start = ((), (), s32[]{:S(2)}) async-start(), calls=%async_computation.1 | async-start | bytes 11053056 | tf_op jit(solution)/shard_map/all_gather | solution.py:102
  10.5 325.1 %all-to-all-start = ((f32[4,1,3]{2,1,0:T(1,128)}), f32[4,1,3]{2,1,0:T(1,128)S(1)}, u32[]{:S(2)}, u32[]{:S(2)}) async-start(f32[4,1,3]{2,1,0:T(1,128)} %broadcast_in_dim.49), calls=%async_computation | async-start | bytes 4096 | tf_op jit(solution)/shard_map/all_to_all | solution.py:24
  365.1 140.5 %copy-start = (f32[1,3]{1,0:T(1,128)S(1)}, f32[1,3]{1,0:T(1,128)}, u32[]{:S(2)}) copy-start(f32[1,3]{1,0:T(1,128)} %param.14) | copy-start | bytes 40
  365.1 140.5 %copy-start.1 = (f32[1,3]{1,0:T(1,128)S(1)}, f32[1,3]{1,0:T(1,128)}, u32[]{:S(2)}) copy-start(f32[1,3]{1,0:T(1,128)} %param.15) | copy-start | bytes 40
Sparse Core Ops, SparseCore 0:
  12.2 286.0 all-gather.2
where the time goes:
time: 605 us; the launch traced here: 603 us
  blocking collectives  520 us (86%)
  local copies, waits for them, and re-layouts  38.3 us (6%)
  between operations  22.4 us (4%)
  other arithmetic  13.4 us (2%)
    all_gather x1, blocking collectives, sent_together(): lax.all_gather(both, axis, axis=dim, tiled=True)  304 us
    psum x7, blocking collectives, by_axis(): array = lax.psum(array, axis)  152 us
    pmax x3, blocking collectives, over_axes(): array = lax.pmax(array, axis)  63.2 us
    gather x1, local copies, waits for them, and re-layouts, local(): packed_rows = rows_flat[row_order]  14.2 us
  transfers between devices with their start and end apart: 2, of which 0 were waited for; matrix products, arithmetic and copies ran while one was open for 3% of the time, Pallas kernels for 0%

commit v1 on v0

v1 whole, which is shorter than its diff:
```python
import jax
import jax.numpy as jnp
from jax import lax
from jax.experimental import pallas as pl
from jax.experimental.pallas import tpu as pltpu
from jax.sharding import Mesh
from jax.sharding import PartitionSpec as P

FAR = 8
NEAR = 4
ROW = ("zh", "zn", "c", "y")
PROMPT = ("zh", "zn", "c")
Z = ("zh", "zn")
PLANE = ("c", "x", "y")

clip_low = 0.8
clip_high = 1.2
dual_clip = 3.0
kl_weight = 0.04
reward_unit = 0.01
std_floor = 0.5


def from_everyone(array, axis):
    devices = lax.axis_size(axis)
    return lax.all_to_all(
        jnp.broadcast_to(array[None], (devices, *array.shape)), axis, 0, 0, tiled=True
    )


def stats_kernel(x_ref, w_ref, ids_ref, out_ref):
    groups, _, per = out_ref.shape
    logits = lax.dot_general(
        w_ref[...], x_ref[...], (((1,), (1,)), ((), ())), preferred_element_type=jnp.float32
    )
    peak = jnp.max(logits, axis=0, keepdims=True)
    total = jnp.sum(jnp.exp(logits - peak), axis=0, keepdims=True)
    line = lax.broadcasted_iota(jnp.int32, logits.shape, 0)
    target = jnp.sum(jnp.where(line == ids_ref[...], logits, 0.0), axis=0, keepdims=True)
    for g in range(groups):
        out_ref[g, 0:1, :] = peak[:, g * per : (g + 1) * per]
        out_ref[g, 1:2, :] = total[:, g * per : (g + 1) * per]
        out_ref[g, 2:3, :] = target[:, g * per : (g + 1) * per]


def shard_stats(rows, weight, local_ids, groups):
    count, width = rows.shape
    vocab = weight.shape[0]
    return pl.pallas_call(
        stats_kernel,
        out_shape=jax.ShapeDtypeStruct((groups, 3, count // groups), jnp.float32),
        cost_estimate=pl.CostEstimate(
            flops=2 * count * width * vocab,
            bytes_accessed=2 * width * (count + vocab),
            transcendentals=count * vocab,
        ),
        name="shard_stats",
    )(rows, weight, local_ids)


def merged(stats):
    peak = jnp.max(stats[:, 0], axis=0)
    total = jnp.sum(stats[:, 1] * jnp.exp(stats[:, 0] - peak), axis=0)
    target = jnp.sum(stats[:, 2], axis=0)
    return jnp.stack([peak, total, target])


def local(
    hidden, unembed, token_ids, old_logp, ref_logp, loss_mask, lengths, sample_valid, rewards
):
    _, local_rows, width = hidden.shape
    vocab_rows = unembed.shape[0]
    n_y = lax.axis_size("y")
    n_z = lax.axis_size(Z)
    column_rows = n_z * local_rows
    core = lax.axis_index("c")

    far = from_everyone(hidden.reshape(local_rows * width // 128, 128), "zh")
    near = from_everyone(far, "zn")
    rows = (
        near.reshape(NEAR, FAR, local_rows, width)
        .transpose(1, 0, 2, 3)
        .reshape(column_rows, width)
    )
    own = from_everyone(rows, "y").reshape(n_y * column_rows, width)
    other = lax.ppermute(own, "c", [(0, 1), (1, 0)])

    positions = lax.axis_index("y") * local_rows + lax.broadcasted_iota(
        jnp.int32, (1, local_rows), 1
    )
    live_rows = (loss_mask == 1) & (positions < lengths.T) & (sample_valid.T == 1)
    valid_f = sample_valid.astype(jnp.float32)
    scores = rewards.astype(jnp.float32) * reward_unit
    moments = from_everyone(
        jnp.concatenate([valid_f, valid_f * scores, valid_f * scores * scores], axis=1), "x"
    )
    group_count, first_moment, second_moment = jnp.split(jnp.sum(moments, axis=0), 3, axis=1)
    safe_count = jnp.maximum(group_count, 1.0)
    group_mean = first_moment / safe_count
    spread = jnp.sqrt(jnp.maximum(second_moment / safe_count - group_mean * group_mean, 0.0))
    advantages = valid_f * (scores - group_mean) / jnp.maximum(spread, std_floor)

    side = jnp.concatenate(
        [
            token_ids.astype(jnp.float32),
            old_logp,
            ref_logp,
            live_rows.astype(jnp.float32),
            jnp.broadcast_to(advantages, (1, local_rows)),
        ]
    )
    side = from_everyone(side, Z).transpose(1, 0, 2).reshape(5, column_rows)
    vocab_start = lax.axis_index(ROW) * vocab_rows
    all_ids = from_everyone(side[0:1].astype(jnp.int32), ("c", "y")) - vocab_start
    all_ids = all_ids.reshape(2, n_y * column_rows)
    own_ids = lax.dynamic_slice_in_dim(all_ids, core, 1, 0)
    other_ids = lax.dynamic_slice_in_dim(all_ids, 1 - core, 1, 0)

    own_stats = shard_stats(own, unembed, own_ids, n_y)
    other_stats = shard_stats(other, unembed, other_ids, n_y)
    low = jnp.where(core == 0, own_stats, other_stats)
    high = jnp.where(core == 0, other_stats, own_stats)
    plane = lax.all_to_all(jnp.concatenate([low, high]), ("c", "y"), 0, 0, tiled=True)
    total = merged(from_everyone(merged(plane), Z))
    raw_logp = total[2:3] - (total[0:1] + jnp.log(total[1:2]))

    live = side[3:4] > 0.5
    adv_rows = side[4:5]
    token_logp = jnp.where(live, raw_logp, 0.0)
    prob_ratio = jnp.exp(raw_logp - side[1:2])
    gain_side = adv_rows * jnp.minimum(prob_ratio, clip_high)
    loss_side = jnp.maximum(adv_rows * jnp.maximum(prob_ratio, clip_low), dual_clip * adv_rows)
    objective = jnp.where(adv_rows >= 0.0, gain_side, loss_side)
    log_gap = side[2:3] - raw_logp
    kl_term = jnp.exp(log_gap) - log_gap - 1.0
    token_loss = jnp.where(live, kl_weight * kl_term - objective, 0.0)
    sums = jnp.stack([jnp.sum(token_loss), jnp.sum(side[3:4])])
    sums = jnp.sum(from_everyone(sums, PLANE), axis=0)
    loss = sums[0] / jnp.maximum(sums[1], 1.0)
    start = lax.axis_index(Z) * local_rows
    return (
        lax.dynamic_slice_in_dim(token_logp, start, local_rows, 1),
        lax.dynamic_slice_in_dim(token_loss, start, local_rows, 1),
        advantages,
        loss,
    )


def solution(mesh):
    split = Mesh(
        mesh.devices.reshape(FAR, NEAR, 2, mesh.shape["sample"], mesh.shape["vocab"]),
        ("zh", "zn", "c", "x", "y"),
    )
    in_specs = (
        P("x", ROW, None),
        P(ROW, None),
        P("x", ROW),
        P("x", ROW),
        P("x", ROW),
        P("x", ROW),
        P(PROMPT, "x"),
        P(PROMPT, "x"),
        P(PROMPT, "x"),
    )
    out_specs = (P("x", ROW), P("x", ROW), P(PROMPT, "x"), P())
    return jax.shard_map(local, mesh=split, in_specs=in_specs, out_specs=out_specs, check_vma=False)
```

time: 605 us -> 251 us (0.41)
  blocking collectives: 520 us -> 154 us
  waiting for transfers between devices: 0.04 us -> 38.4 us
  local copies, waits for them, and re-layouts: 38.3 us -> 8.52 us
  starting transfers between devices: 4.87 us -> 25.5 us
  between operations: 22.4 us -> 8.48 us
  Pallas kernels: 0 us -> 12.7 us
  other arithmetic: 13.4 us -> 3.08 us
    all_gather x1 -> x0, blocking collectives: 304 us -> none  [sent_together(): lax.all_gather(both, axis, axis=dim, tiled=True)]
    all_to_all x0 -> x5, blocking collectives: none -> 154 us  [the longest x4 146 us: from_everyone(): lax.all_to_all(jnp.broadcast_to(array[None], (devices, *array.shape)), ax...]
    psum x7 -> x0, blocking collectives: 152 us -> none  [by_axis(): array = lax.psum(array, axis)]
    pmax x3 -> x0, blocking collectives: 63.2 us -> none  [over_axes(): array = lax.pmax(array, axis)]
    all_to_all x1 -> x4, waiting for transfers between devices: 0.01 us -> 38.4 us  [from_everyone(): lax.all_to_all(jnp.broadcast_to(array[None], (devices, *array.shape)), ax...]
    gather x5 -> x0, local copies, waits for them, and re-layouts: 27 us -> none  [the longest x1 14.2 us: local(): packed_rows = rows_flat[row_order]]
    all_to_all x1 -> x4, starting transfers between devices: 4.83 us -> 20.3 us  [from_everyone(): lax.all_to_all(jnp.broadcast_to(array[None], (devices, *array.shape)), ax...]
    pallas_call x0 -> x2, Pallas kernels: none -> 12.7 us  [shard_stats(): pl.pallas_call(stats_kernel, out_shape=jax.ShapeDtypeStruct((groups, 3, c...]
  transfers between devices with their start and end apart: 2 -> 5, of which waited for: 0 -> 4; matrix products, arithmetic and copies ran while one was open for 3% -> 2% of each run, Pallas kernels for 0% -> 3%
where the time goes in v1:
time: 251 us; the launch traced here: 250 us
  blocking collectives  154 us (61%)
  waiting for transfers between devices  38.4 us (15%)
  starting transfers between devices  25.5 us (10%)
  Pallas kernels  12.7 us (5%)
  local copies, waits for them, and re-layouts  8.52 us (3%)
  between operations  8.48 us (3%)
  other arithmetic  3.08 us (1%)
    all_to_all x4, blocking collectives, from_everyone(): lax.all_to_all(jnp.broadcast_to(array[None], (devices, *array.shape)), ax...  146 us
    all_to_all x4, waiting for transfers between devices, from_everyone(): lax.all_to_all(jnp.broadcast_to(array[None], (devices, *array.shape)), ax...  38.4 us
    all_to_all x4, starting transfers between devices, from_everyone(): lax.all_to_all(jnp.broadcast_to(array[None], (devices, *array.shape)), ax...  20.3 us
    pallas_call x2, Pallas kernels, shard_stats(): pl.pallas_call(stats_kernel, out_shape=jax.ShapeDtypeStruct((groups, 3, c...  12.7 us
    all_to_all x1, blocking collectives, local(): lax.all_to_all(jnp.concatenate([low, high]), ('c', 'y'), 0, 0, tiled=True)  7.93 us
    ppermute x1, starting transfers between devices, local(): other = lax.ppermute(own, 'c', [(0, 1), (1, 0)])  5.23 us
  transfers between devices with their start and end apart: 5, of which 4 were waited for; matrix products, arithmetic and copies ran while one was open for 2% of the time, Pallas kernels for 3%

profile of v1, /device:TPU:1, one launch (start us, length us, event | category | flops | bytes accessed | tf_op | source)
XLA Modules:
  0.0 250.4 jit_solution(10128767491908008202)
XLA Ops:
  0.6 0.8 broadcast_in_dim.73
  1.4 55.7 %all_to_all.46 = bf16[8,84,128]{2,1,0:T(8,128)(2,1)S(1)} all-to-all(bf16[8,84,128]{2,1,0:T(8,128)(2,1)S(1)} %broadcast_in_dim.74), channel_id=1, replica_groups=mesh['zh'=8,'zn'=4,'c'=2,'x'=4,'y'=4] {'zh'}, dimensions={0} | all-to-all | bytes 344064 | tf_op jit(solution)/shard_map/all_to_all | solution.py:26
  57.2 26.1 %all_to_all.47 = bf16[4,8,84,128]{3,1,2,0:T(8,128)(2,1)S(1)} all-to-all(bf16[4,8,84,128]{3,1,2,0:T(8,128)(2,1)S(1)} %broadcast_in_dim.75), channel_id=1, replica_groups=mesh['zh'=8,'zn'=4,'c'=2,'x'=4,'y'=4] {'zn'}, dimensions={0} | all-to-all | bytes 1376256 | tf_op jit(solution)/shard_map/all_to_all | solution.py:26
  84.1 0.6 broadcast_in_dim.76
  85.0 35.1 %all_to_all.48 = bf16[4,96,3584]{2,1,0:T(8,128)(2,1)S(1)} all-to-all(bf16[4,96,3584]{2,1,0:T(8,128)(2,1)S(1)} %broadcast_in_dim.77), channel_id=1, replica_groups=mesh['zh'=8,'zn'=4,'c'=2,'x'=4,'y'=4] {'y'}, dimensions={0} | all-to-all | bytes 5505024 | tf_op jit(solution)/shard_map/all_to_all | solution.py:26
  120.0 5.2 %collective-permute-start = (bf16[384,3584]{1,0:T(8,128)(2,1)S(1)}, bf16[384,3584]{1,0:T(8,128)(2,1)}, u32[]{:S(2)}, u32[]{:S(2)}) collective-permute-start(bf16[384,3584]{1,0:T(8,128)(2,1)S(1)} %bitcast.35), channel_id=1, source_target_pairs={{0,16},{16,0},{1,17},{17,1},{2,18},{18,2},{3,19},{19,3},{4,20},{20... | collective-permute-start | bytes 8257544 | tf_op jit(solution)/shard_map/ppermute | solution.py:86
  127.3 4.0 %all-to-all-start = ((f32[4,1,3]{2,1,0:T(1,128)}), f32[4,1,3]{2,1,0:T(1,128)S(1)}, u32[]{:S(2)}, u32[]{:S(2)}) async-start(f32[4,1,3]{2,1,0:T(1,128)} %broadcast_in_dim.34), calls=%async_computation | async-start | bytes 4096 | tf_op jit(solution)/shard_map/all_to_all | solution.py:26
  132.0 3.3 %all-to-all-done = f32[4,1,3]{2,1,0:T(1,128)S(1)} async-done(((f32[4,1,3]{2,1,0:T(1,128)}), f32[4,1,3]{2,1,0:T(1,128)S(1)}, u32[]{:S(2)}, u32[]{:S(2)}) %all-to-all-start) | async-done | bytes 80 | tf_op jit(solution)/shard_map/all_to_all | solution.py:26
  138.1 29.0 %all_to_all.49 = f32[32,5,3]{1,2,0:T(4,128)S(1)} all-to-all(f32[32,5,3]{1,2,0:T(4,128)S(1)} %broadcast_in_dim.72), channel_id=1, replica_groups=mesh['zh'=8,'zn'=4,'c'=2,'x'=4,'y'=4] {'zh','zn'}, dimensions={0} | all-to-all | bytes 3840 | tf_op jit(solution)/shard_map/all_to_all | solution.py:26
  167.5 0.6 broadcast_in_dim.78
  168.1 6.6 %all-to-all-start.5 = ((s32[8,1,96]{2,1,0:T(1,128)}), s32[8,1,96]{2,1,0:T(1,128)S(1)}, u32[]{:S(2)}, u32[]{:S(2)}) async-start(s32[8,1,96]{2,1,0:T(1,128)} %broadcast_in_dim.78), calls=%async_computation.5 | async-start | bytes 8192 | tf_op jit(solution)/shard_map/all_to_all | solution.py:26
  174.7 4.6 %all-to-all-done.5 = s32[8,1,96]{2,1,0:T(1,128)S(1)} async-done(((s32[8,1,96]{2,1,0:T(1,128)}), s32[8,1,96]{2,1,0:T(1,128)S(1)}, u32[]{:S(2)}, u32[]{:S(2)}) %all-to-all-start.5) | async-done | bytes 3104 | tf_op jit(solution)/shard_map/all_to_all | solution.py:26
  180.0 6.3 %shard_stats.2 = f32[4,3,96]{2,1,0:T(4,128)} custom-call(bf16[384,3584]{1,0:T(8,128)(2,1)} %bitcast.36, bf16[594,3584]{1,0:T(8,128)(2,1)} %w_ref.3, s32[1,384]{1,0:T(1,128)} %get-tuple-element.19.ids_ref), custom_call_target="tpu_custom_call" | custom-call | flops 1634992128 | bytes 7010304 | tf_op jit(solution)/shard_map/shard_stats/pallas_call | solution.py:49
  186.3 6.3 %shard_stats.3 = f32[4,3,96]{2,1,0:T(4,128)} custom-call(bf16[384,3584]{1,0:T(8,128)(2,1)} %collective-permute-done.x_ref, bf16[594,3584]{1,0:T(8,128)(2,1)} %w_ref.3, s32[1,384]{1,0:T(1,128)} %get-tuple-element.20.ids_ref), custom_call_target="tpu_custom_call" | custom-call | flops 1634992128 | bytes 7010304 | tf_op jit(solution)/shard_map/shard_stats/pallas_call | solution.py:49
  192.7 0.7 broadcast_select_fusion.1
  193.4 7.9 %all_to_all.50 = f32[8,3,96]{2,1,0:T(4,128)S(1)} all-to-all(f32[8,3,96]{2,1,0:T(4,128)S(1)} %pad_maximum_fusion), channel_id=1, replica_groups=mesh['zh'=8,'zn'=4,'c'=2,'x'=4,'y'=4] {'c','y'}, dimensions={0} | all-to-all | bytes 18432 | tf_op jit(solution)/shard_map/all_to_all | solution.py:123
  201.4 0.6 broadcast_in_dim.79
  202.0 3.9 %all-to-all-start.7 = ((f32[32,3,96]{2,1,0:T(4,128)}), f32[32,3,96]{2,1,0:T(4,128)S(1)}, u32[]{:S(2)}, u32[]{:S(2)}) async-start(f32[32,3,96]{2,1,0:T(4,128)} %broadcast_in_dim.79), calls=%async_computation.7 | async-start | bytes 131072 | tf_op jit(solution)/shard_map/all_to_all | solution.py:26
  206.2 24.3 %all-to-all-done.7 = f32[32,3,96]{2,1,0:T(4,128)S(1)} async-done(((f32[32,3,96]{2,1,0:T(4,128)}), f32[32,3,96]{2,1,0:T(4,128)S(1)}, u32[]{:S(2)}, u32[]{:S(2)}) %all-to-all-start.7) | async-done | bytes 36896 | tf_op jit(solution)/shard_map/all_to_all | solution.py:26
  230.7 0.6 fusion.4
  231.5 1.4 pad_maximum_fusion.2
  232.8 0.6 broadcast_in_dim.82
  233.4 5.9 %all-to-all-start.8 = ((f32[32,1,2]{2,1,0:T(1,128)}), f32[32,1,2]{2,1,0:T(1,128)S(1)}, u32[]{:S(2)}, u32[]{:S(2)}) async-start(f32[32,1,2]{2,1,0:T(1,128)} %broadcast_in_dim.82), calls=%async_computation.8 | async-start | bytes 32768 | tf_op jit(solution)/shard_map/all_to_all | solution.py:26
  239.9 6.2 %all-to-all-done.8 = f32[32,1,2]{2,1,0:T(1,128)S(1)} async-done(((f32[32,1,2]{2,1,0:T(1,128)}), f32[32,1,2]{2,1,0:T(1,128)S(1)}, u32[]{:S(2)}, u32[]{:S(2)}) %all-to-all-start.8) | async-done | bytes 288 | tf_op jit(solution)/shard_map/all_to_all | solution.py:26
  (55 shorter events, 5.7 us)
Async XLA Ops:
  84.9 47.0 %copy-start.5 = (s32[1,3]{1,0:T(1,128)S(1)}, s32[1,3]{1,0:T(1,128)}, u32[]{:S(2)}) copy-start(s32[1,3]{1,0:T(1,128)} %param.11) | copy-start | bytes 40
  84.9 47.0 %copy-start.2 = (s32[1,3]{1,0:T(1,128)S(1)}, s32[1,3]{1,0:T(1,128)}, u32[]{:S(2)}) copy-start(s32[1,3]{1,0:T(1,128)} %param.14) | copy-start | bytes 40
  84.9 53.0 %copy-start.3 = (f32[1,3]{1,0:T(1,128)S(1)}, f32[1,3]{1,0:T(1,128)}, u32[]{:S(2)}) copy-start(f32[1,3]{1,0:T(1,128)} %param.12) | copy-start | bytes 40
  84.9 53.0 %copy-start.4 = (f32[1,3]{1,0:T(1,128)S(1)}, f32[1,3]{1,0:T(1,128)}, u32[]{:S(2)}) copy-start(f32[1,3]{1,0:T(1,128)} %param.13) | copy-start | bytes 40
  120.0 59.9 %copy-start = (bf16[4,96,3584]{2,1,0:T(8,128)(2,1)}, bf16[4,96,3584]{2,1,0:T(8,128)(2,1)S(1)}, u32[]{:S(2)}) copy-start(bf16[4,96,3584]{2,1,0:T(8,128)(2,1)S(1)} %all_to_all.48) | copy-start | bytes 8257540
  120.0 66.3 %collective-permute-start = (bf16[384,3584]{1,0:T(8,128)(2,1)S(1)}, bf16[384,3584]{1,0:T(8,128)(2,1)}, u32[]{:S(2)}, u32[]{:S(2)}) collective-permute-start(bf16[384,3584]{1,0:T(8,128)(2,1)S(1)} %bitcast.35), channel_id=1, source_target_pairs={{0,16},{16,0},{1,17},{17,1},{2,18},{18,2},{3,19},{19,3},{4,20},{20... | collective-permute-start | bytes 8257544 | tf_op jit(solution)/shard_map/ppermute | solution.py:86
  127.3 8.0 %all-to-all-start = ((f32[4,1,3]{2,1,0:T(1,128)}), f32[4,1,3]{2,1,0:T(1,128)S(1)}, u32[]{:S(2)}, u32[]{:S(2)}) async-start(f32[4,1,3]{2,1,0:T(1,128)} %broadcast_in_dim.34), calls=%async_computation | async-start | bytes 4096 | tf_op jit(solution)/shard_map/all_to_all | solution.py:26
  168.1 11.2 %all-to-all-start.5 = ((s32[8,1,96]{2,1,0:T(1,128)}), s32[8,1,96]{2,1,0:T(1,128)S(1)}, u32[]{:S(2)}, u32[]{:S(2)}) async-start(s32[8,1,96]{2,1,0:T(1,128)} %broadcast_in_dim.78), calls=%async_computation.5 | async-start | bytes 8192 | tf_op jit(solution)/shard_map/all_to_all | solution.py:26
  186.3 6.4 %copy-start.1 = (f32[4,3,96]{2,1,0:T(4,128)S(1)}, f32[4,3,96]{2,1,0:T(4,128)}, u32[]{:S(2)}) copy-start(f32[4,3,96]{2,1,0:T(4,128)} %shard_stats.2) | copy-start | bytes 13828
  202.0 28.5 %all-to-all-start.7 = ((f32[32,3,96]{2,1,0:T(4,128)}), f32[32,3,96]{2,1,0:T(4,128)S(1)}, u32[]{:S(2)}, u32[]{:S(2)}) async-start(f32[32,3,96]{2,1,0:T(4,128)} %broadcast_in_dim.79), calls=%async_computation.7 | async-start | bytes 131072 | tf_op jit(solution)/shard_map/all_to_all | solution.py:26
  233.4 12.7 %all-to-all-start.8 = ((f32[32,1,2]{2,1,0:T(1,128)}), f32[32,1,2]{2,1,0:T(1,128)S(1)}, u32[]{:S(2)}, u32[]{:S(2)}) async-start(f32[32,1,2]{2,1,0:T(1,128)} %broadcast_in_dim.82), calls=%async_computation.8 | async-start | bytes 32768 | tf_op jit(solution)/shard_map/all_to_all | solution.py:26

commit v2 on v1

v2 whole, which is shorter than its diff:
```python
import jax
import jax.numpy as jnp
from jax import lax
from jax.experimental import pallas as pl
from jax.experimental.pallas import tpu as pltpu
from jax.sharding import Mesh
from jax.sharding import PartitionSpec as P


ROW = ("z", "c", "y")
PROMPT = ("z", "c")
PLANE = ("c", "x", "y")
LANES = 128
KERNEL_VMEM = 24 * 2**20

clip_low = 0.8
clip_high = 1.2
dual_clip = 3.0
kl_weight = 0.04
reward_unit = 0.01
std_floor = 0.5


def from_everyone(array, axis):
    devices = lax.axis_size(axis)
    return lax.all_to_all(
        jnp.broadcast_to(array[None], (devices, *array.shape)), axis, 0, 0, tiled=True
    )


def split_exact(values):
    pieces = []
    for _ in range(3):
        piece = lax.reduce_precision(values, 8, 7)
        pieces.append(piece.astype(jnp.bfloat16))
        values = values - piece
    return pieces


def stats_kernel(start_ref, x_ref, own_ref, other_ref, out_ref):
    groups, _, per = out_ref.shape
    vocab, width = own_ref.shape
    rows = x_ref[:, :width]
    side = x_ref[:, width:]
    pick = (lax.broadcasted_iota(jnp.int32, (8, LANES), 1) < 3).astype(jnp.bfloat16)
    contract = (((1,), (1,)), ((), ()))
    ids = lax.dot_general(pick, side, contract, preferred_element_type=jnp.float32)
    ids = ids[0:1].astype(jnp.int32)
    line = lax.broadcasted_iota(jnp.int32, (vocab, rows.shape[0]), 0)
    parts = []
    for half, w_ref in enumerate((own_ref, other_ref)):
        logits = lax.dot_general(w_ref[...], rows, contract, preferred_element_type=jnp.float32)
        peak = jnp.max(logits, axis=0, keepdims=True)
        total = jnp.sum(jnp.exp(logits - peak), axis=0, keepdims=True)
        hit = line == ids - start_ref[half]
        parts.append((peak, total, jnp.sum(jnp.where(hit, logits, 0.0), axis=0, keepdims=True)))
    (peak_a, total_a, target_a), (peak_b, total_b, target_b) = parts
    peak = jnp.maximum(peak_a, peak_b)
    total = total_a * jnp.exp(peak_a - peak) + total_b * jnp.exp(peak_b - peak)
    lse = peak + jnp.log(total)
    target = target_a + target_b
    for g in range(groups):
        out_ref[g, 0:1, :] = lse[:, g * per : (g + 1) * per]
        out_ref[g, 1:2, :] = target[:, g * per : (g + 1) * per]


def shard_stats(rows, own, other, starts, groups):
    count = rows.shape[0]
    vocab, width = own.shape
    return pl.pallas_call(
        stats_kernel,
        in_specs=[
            pl.BlockSpec(memory_space=pltpu.SMEM),
            pl.BlockSpec(memory_space=pltpu.VMEM),
            pl.BlockSpec(memory_space=pltpu.VMEM),
            pl.BlockSpec(memory_space=pltpu.VMEM),
        ],
        out_specs=pl.BlockSpec(memory_space=pltpu.VMEM),
        out_shape=jax.ShapeDtypeStruct((groups, 2, count // groups), jnp.float32),
        cost_estimate=pl.CostEstimate(
            flops=4 * count * width * vocab,
            bytes_accessed=2 * width * (count + 2 * vocab),
            transcendentals=2 * count * vocab,
        ),
        compiler_params=pltpu.CompilerParams(vmem_limit_bytes=KERNEL_VMEM),
        name="shard_stats",
    )(starts, rows, own, other)


def merged(lse):
    peak = jnp.max(lse, axis=0)
    return peak + jnp.log(jnp.sum(jnp.exp(lse - peak), axis=0))


def group_advantages(sums, valid_f, scores):
    group_count, first_moment, second_moment = (sums[i : i + 1] for i in range(3))
    safe_count = jnp.maximum(group_count, 1.0)
    group_mean = first_moment / safe_count
    spread = jnp.sqrt(jnp.maximum(second_moment / safe_count - group_mean * group_mean, 0.0))
    return valid_f * (scores - group_mean) / jnp.maximum(spread, std_floor)


def local(
    hidden, unembed, token_ids, old_logp, ref_logp, loss_mask, lengths, sample_valid, rewards
):
    _, local_rows, width = hidden.shape
    vocab_rows = unembed.shape[0]
    n_x = lax.axis_size("x")
    n_y = lax.axis_size("y")
    n_z = lax.axis_size("z")
    column_rows = n_z * local_rows
    core = lax.axis_index("c")

    positions = lax.axis_index("y") * local_rows + lax.broadcasted_iota(
        jnp.int32, (1, local_rows), 1
    )
    live_rows = (loss_mask == 1) & (positions < lengths.T) & (sample_valid.T == 1)
    fields = jnp.concatenate(
        [
            token_ids.astype(jnp.float32),
            old_logp,
            ref_logp,
            live_rows.astype(jnp.float32),
            jnp.broadcast_to(sample_valid.astype(jnp.float32), (1, local_rows)),
            jnp.broadcast_to(rewards.astype(jnp.float32), (1, local_rows)),
        ]
    )
    n_fields = fields.shape[0]
    pieces = jnp.stack(split_exact(fields.T), axis=2).reshape(local_rows, 3 * n_fields)
    pieces = jnp.pad(pieces, ((0, 0), (0, LANES - 3 * n_fields)))
    full = width + LANES
    chunk = jnp.concatenate([hidden[0], pieces], axis=1).reshape(local_rows * full // LANES, LANES)
    tall = -(-chunk.shape[0] // 8) * 8
    column = lax.all_gather(jnp.pad(chunk, ((0, tall - chunk.shape[0]), (0, 0))), "z", axis=0)
    rows = column[:, : chunk.shape[0]].reshape(column_rows, full)

    other_unembed = lax.ppermute(unembed, "c", [(0, 1), (1, 0)])
    gathered = from_everyone(rows, "y").reshape(n_y * column_rows, full)

    side = rows[:, width : width + 3 * n_fields].astype(jnp.float32).T
    side = side.reshape(n_fields, 3, column_rows)
    side = side[:, 0] + side[:, 1] + side[:, 2]
    old_rows, ref_rows, live_float, valid_f, reward_rows = (side[i : i + 1] for i in range(1, 6))
    scores = reward_rows * reward_unit
    moments = jnp.concatenate([valid_f, valid_f * scores, valid_f * scores * scores])
    terms = [moments]
    for d in range(1, n_x):
        ring = [(i, (i + d) % n_x) for i in range(n_x)]
        terms.append(lax.ppermute(moments, "x", ring))
    adv_rows = group_advantages(sum(terms), valid_f, scores)
    z = lax.axis_index("z")
    shards = jnp.stack([(z * 2 + core) * n_y, (z * 2 + 1 - core) * n_y]) + lax.axis_index("y")
    stats = shard_stats(gathered, unembed, other_unembed, shards * vocab_rows, n_y)
    plane = lax.all_to_all(stats, "y", 0, 0, tiled=True)
    plane = jnp.concatenate([merged(plane[:, 0:1]), jnp.sum(plane[:, 1:2], axis=0)])
    back = from_everyone(plane, "z")
    raw_logp = jnp.sum(back[:, 1:2], axis=0) - merged(back[:, 0:1])

    live = live_float > 0.5
    token_logp = jnp.where(live, raw_logp, 0.0)
    prob_ratio = jnp.exp(raw_logp - old_rows)
    gain_side = adv_rows * jnp.minimum(prob_ratio, clip_high)
    loss_side = jnp.maximum(adv_rows * jnp.maximum(prob_ratio, clip_low), dual_clip * adv_rows)
    objective = jnp.where(adv_rows >= 0.0, gain_side, loss_side)
    log_gap = ref_rows - raw_logp
    kl_term = jnp.exp(log_gap) - log_gap - 1.0
    token_loss = jnp.where(live, kl_weight * kl_term - objective, 0.0)
    totals = jnp.stack([jnp.sum(token_loss), jnp.sum(live_float)])
    totals = jnp.sum(from_everyone(totals, PLANE), axis=0)
    loss = totals[0] / jnp.maximum(totals[1], 1.0)
    first = z * local_rows
    return (
        lax.dynamic_slice_in_dim(token_logp, first, local_rows, 1),
        lax.dynamic_slice_in_dim(token_loss, first, local_rows, 1),
        lax.dynamic_slice_in_dim(adv_rows, first, 1, 1),
        loss,
    )


def solution(mesh):
    split = Mesh(
        mesh.devices.reshape(
            mesh.shape["prompt"] // 2, 2, mesh.shape["sample"], mesh.shape["vocab"]
        ),
        ("z", "c", "x", "y"),
    )
    in_specs = (
        P("x", ROW, None),
        P(ROW, None),
        P("x", ROW),
        P("x", ROW),
        P("x", ROW),
        P("x", ROW),
        P(PROMPT, "x"),
        P(PROMPT, "x"),
        P(PROMPT, "x"),
    )
    out_specs = (P("x", ROW), P("x", ROW), P(PROMPT, "x"), P())
    return jax.shard_map(local, mesh=split, in_specs=in_specs, out_specs=out_specs, check_vma=False)
```

time: 251 us -> 191 us (0.76)
  blocking collectives: 154 us -> 45.7 us
  starting transfers between devices: 25.5 us -> 69.7 us
  waiting for transfers between devices: 38.4 us -> 46.4 us
  Pallas kernels: 12.7 us -> 7.85 us
  between operations: 8.48 us -> 5.22 us
  other arithmetic: 3.08 us -> 5.77 us
    all_to_all x5 -> x0, blocking collectives: 154 us -> none  [the longest x4 146 us: from_everyone(): lax.all_to_all(jnp.broadcast_to(array[None], (devices, *array.shape)), ax...]
    all_gather x0 -> x1, blocking collectives: none -> 45.7 us  [local(): lax.all_gather(jnp.pad(chunk, ((0, tall - chunk.shape[0]), (0, 0))), 'z',...]
    all_to_all x4 -> x3, starting transfers between devices: 20.3 us -> 41.1 us  [from_everyone(): lax.all_to_all(jnp.broadcast_to(array[None], (devices, *array.shape)), ax...]
    ppermute x1 -> x4, starting transfers between devices: 5.23 us -> 25.4 us  [the longest x1 16 us: local(): other_unembed = lax.ppermute(unembed, 'c', [(0, 1), (1, 0)])]
    all_to_all x4 -> x3, waiting for transfers between devices: 38.4 us -> 46.4 us  [from_everyone(): lax.all_to_all(jnp.broadcast_to(array[None], (devices, *array.shape)), ax...]
    pallas_call x2 -> x1, Pallas kernels: 12.7 us -> 7.85 us  [shard_stats(): pl.pallas_call(stats_kernel, in_specs=[pl.BlockSpec(memory_space=pltpu.SM...]
    all_to_all x0 -> x1, starting transfers between devices: none -> 3.22 us  [local(): plane = lax.all_to_all(stats, 'y', 0, 0, tiled=True)]
  transfers between devices with their start and end apart: 5 -> 8, of which waited for: 4 -> 3; matrix products, arithmetic and copies ran while one was open for 2% -> 5% of each run, Pallas kernels for 3% -> 0%
where the time goes in v2:
time: 191 us; the launch traced here: 190 us
  starting transfers between devices  69.7 us (36%)
  waiting for transfers between devices  46.4 us (24%)
  blocking collectives  45.7 us (24%)
  local copies, waits for them, and re-layouts  9.17 us (5%)
  Pallas kernels  7.85 us (4%)
  other arithmetic  5.77 us (3%)
  between operations  5.22 us (3%)
    all_to_all x3, waiting for transfers between devices, from_everyone(): lax.all_to_all(jnp.broadcast_to(array[None], (devices, *array.shape)), ax...  46.4 us
    all_gather x1, blocking collectives, local(): lax.all_gather(jnp.pad(chunk, ((0, tall - chunk.shape[0]), (0, 0))), 'z',...  45.7 us
    all_to_all x3, starting transfers between devices, from_everyone(): lax.all_to_all(jnp.broadcast_to(array[None], (devices, *array.shape)), ax...  41.1 us
    ppermute x1, starting transfers between devices, local(): other_unembed = lax.ppermute(unembed, 'c', [(0, 1), (1, 0)])  16 us
    ppermute x3, starting transfers between devices, local(): terms.append(lax.ppermute(moments, 'x', ring))  9.33 us
    pallas_call x1, Pallas kernels, shard_stats(): pl.pallas_call(stats_kernel, in_specs=[pl.BlockSpec(memory_space=pltpu.SM...  7.85 us
  transfers between devices with their start and end apart: 8, of which 3 were waited for; matrix products, arithmetic and copies ran while one was open for 5% of the time, Pallas kernels for 0%

profile of v2, /device:TPU:1, one launch (start us, length us, event | category | flops | bytes accessed | tf_op | source)
XLA Modules:
  0.0 189.8 jit_solution(8743025432665736513)
XLA Ops:
  0.6 16.0 %collective-permute-start = (bf16[594,3584]{1,0:T(8,128)(2,1)}, bf16[594,3584]{1,0:T(8,128)(2,1)}, u32[]{:S(2)}, u32[]{:S(2)}) collective-permute-start(bf16[594,3584]{1,0:T(8,128)(2,1)} %own_ref.1), channel_id=1, source_target_pairs={{0,16},{16,0},{1,17},{17,1},{2,18},{18,2},{3,19},{19,3},{4,20},{20... | collective-permute-start | bytes 12773384 | tf_op jit(solution)/shard_map/ppermute | solution.py:137
  16.7 0.7 convert_element_type.26
  19.3 0.7 and_convert_fusion
  19.9 0.7 concatenate.12
  21.2 0.8 fusion.1
  22.0 45.7 %all-gather = bf16[2816,128]{1,0:T(8,128)(2,1)S(1)} all-gather(bf16[88,128]{1,0:T(8,128)(2,1)S(1)} %pad.9), channel_id=2, replica_groups=mesh['z'=32,'c'=2,'x'=4,'y'=4] {'z'}, dimensions={0}, use_global_device_ids=true | all-gather | bytes 743424 | tf_op jit(solution)/shard_map/all_gather | solution.py:134
  67.7 0.8 reshape.129
  68.5 1.8 broadcast_in_dim.42
  70.3 4.2 %all-to-all-start = ((bf16[4,96,3712]{2,1,0:T(8,128)(2,1)}), bf16[4,96,3712]{2,1,0:T(8,128)(2,1)S(1)}, u32[]{:S(2)}, u32[]{:S(2)}) async-start(bf16[4,96,3712]{2,1,0:T(8,128)(2,1)} %broadcast_in_dim.42), calls=%async_computation | async-start | bytes 5701632 | tf_op jit(solution)/shard_map/all_to_all | solution.py:26
  74.5 0.7 convert_bitcast_fusion
  76.0 18.7 %all-to-all-done = bf16[4,96,3712]{2,1,0:T(8,128)(2,1)S(1)} async-done(((bf16[4,96,3712]{2,1,0:T(8,128)(2,1)}), bf16[4,96,3712]{2,1,0:T(8,128)(2,1)S(1)}, u32[]{:S(2)}, u32[]{:S(2)}) %all-to-all-start) | async-done | bytes 2850848 | tf_op jit(solution)/shard_map/all_to_all | solution.py:26
  94.8 2.2 %copy-done = bf16[594,3584]{1,0:T(8,128)(2,1)S(1)} copy-done((bf16[594,3584]{1,0:T(8,128)(2,1)S(1)}, bf16[594,3584]{1,0:T(8,128)(2,1)}, u32[]{:S(2)}) %copy-start) | copy-done | bytes 4257816
  97.0 7.8 %shard_stats.1 = f32[4,2,96]{2,1,0:T(2,128)} custom-call(s32[2]{0:T(128)S(1)} %fusion.11.start_ref, bf16[384,3712]{1,0:T(8,128)(2,1)S(1)} %bitcast.76, bf16[594,3584]{1,0:T(8,128)(2,1)S(1)} %copy-done, bf16[594,3584]{1,0:T(8,128)(2,1)} %collective-permute-done.other_ref), custom_call_target="tpu_custom_call" | custom-call | flops 3269984256 | bytes 11268096 | tf_op jit(solution)/shard_map/shard_stats/pallas_call | solution.py:70
  104.9 3.2 %all-to-all-start.1 = ((f32[4,2,96]{2,1,0:T(2,128)}), f32[4,2,96]{2,1,0:T(2,128)S(1)}, u32[]{:S(2)}, u32[]{:S(2)}) async-start(f32[4,2,96]{2,1,0:T(2,128)} %shard_stats.1), calls=%async_computation.1 | async-start | bytes 8192 | tf_op jit(solution)/shard_map/all_to_all | solution.py:154
  108.1 4.4 %collective-permute-start.3 = (f32[3,96]{1,0:T(4,128)S(1)}, f32[3,96]{1,0:T(4,128)S(1)}, u32[]{:S(2)}, u32[]{:S(2)}) collective-permute-start(f32[3,96]{1,0:T(4,128)S(1)} %pad_maximum_fusion.1), channel_id=1, source_target_pairs={{0,12},{4,0},{8,4},{12,8},{1,13},{5,1},{9,5},{13,9},{2,14},{6,2},{... | collective-permute-start | bytes 3464 | tf_op jit(solution)/shard_map/ppermute | solution.py:149
  112.5 2.4 %collective-permute-start.2 = (f32[3,96]{1,0:T(4,128)S(1)}, f32[3,96]{1,0:T(4,128)S(1)}, u32[]{:S(2)}, u32[]{:S(2)}) collective-permute-start(f32[3,96]{1,0:T(4,128)S(1)} %pad_maximum_fusion.1), channel_id=1, source_target_pairs={{0,8},{4,12},{8,0},{12,4},{1,9},{5,13},{9,1},{13,5},{2,10},{6,14},... | collective-permute-start | bytes 3464 | tf_op jit(solution)/shard_map/ppermute | solution.py:149
  114.9 2.5 %collective-permute-start.1 = (f32[3,96]{1,0:T(4,128)S(1)}, f32[3,96]{1,0:T(4,128)S(1)}, u32[]{:S(2)}, u32[]{:S(2)}) collective-permute-start(f32[3,96]{1,0:T(4,128)S(1)} %pad_maximum_fusion.1), channel_id=1, source_target_pairs={{0,4},{4,8},{8,12},{12,0},{1,5},{5,9},{9,13},{13,1},{2,6},{6,10},{... | collective-permute-start | bytes 3464 | tf_op jit(solution)/shard_map/ppermute | solution.py:149
  117.5 0.6 broadcast_in_dim.43
  118.2 12.9 %all-to-all-start.2 = ((f32[32,2,96]{2,1,0:T(2,128)}), f32[32,2,96]{2,1,0:T(2,128)S(1)}, u32[]{:S(2)}, u32[]{:S(2)}) async-start(f32[32,2,96]{2,1,0:T(2,128)} %broadcast_in_dim.43), calls=%async_computation.2 | async-start | bytes 65536 | tf_op jit(solution)/shard_map/all_to_all | solution.py:26
  131.1 22.0 %all-to-all-done.2 = f32[32,2,96]{2,1,0:T(2,128)S(1)} async-done(((f32[32,2,96]{2,1,0:T(2,128)}), f32[32,2,96]{2,1,0:T(2,128)S(1)}, u32[]{:S(2)}, u32[]{:S(2)}) %all-to-all-start.2) | async-done | bytes 24608 | tf_op jit(solution)/shard_map/all_to_all | solution.py:26
  153.1 0.6 fusion.14
  153.8 1.4 pad_maximum_fusion.3
  155.8 24.1 %all-to-all-start.3 = ((f32[32,1,2]{2,1,0:T(1,128)}), f32[32,1,2]{2,1,0:T(1,128)S(1)}, u32[]{:S(2)}, u32[]{:S(2)}) async-start(f32[32,1,2]{2,1,0:T(1,128)} %broadcast_in_dim.45), calls=%async_computation.3 | async-start | bytes 32768 | tf_op jit(solution)/shard_map/all_to_all | solution.py:26
  181.0 5.7 %all-to-all-done.3 = f32[32,1,2]{2,1,0:T(1,128)S(1)} async-done(((f32[32,1,2]{2,1,0:T(1,128)}), f32[32,1,2]{2,1,0:T(1,128)S(1)}, u32[]{:S(2)}, u32[]{:S(2)}) %all-to-all-start.3) | async-done | bytes 288 | tf_op jit(solution)/shard_map/all_to_all | solution.py:26
  (40 shorter events, 4.0 us)
Async XLA Ops:
  0.6 94.2 %collective-permute-start = (bf16[594,3584]{1,0:T(8,128)(2,1)}, bf16[594,3584]{1,0:T(8,128)(2,1)}, u32[]{:S(2)}, u32[]{:S(2)}) collective-permute-start(bf16[594,3584]{1,0:T(8,128)(2,1)} %own_ref.1), channel_id=1, source_target_pairs={{0,16},{16,0},{1,17},{17,1},{2,18},{18,2},{3,19},{19,3},{4,20},{20... | collective-permute-start | bytes 12773384 | tf_op jit(solution)/shard_map/ppermute | solution.py:137
  68.5 1.8 copy-start.1
  70.3 24.5 %all-to-all-start = ((bf16[4,96,3712]{2,1,0:T(8,128)(2,1)}), bf16[4,96,3712]{2,1,0:T(8,128)(2,1)S(1)}, u32[]{:S(2)}, u32[]{:S(2)}) async-start(bf16[4,96,3712]{2,1,0:T(8,128)(2,1)} %broadcast_in_dim.42), calls=%async_computation | async-start | bytes 5701632 | tf_op jit(solution)/shard_map/all_to_all | solution.py:26
  94.8 2.2 %copy-start = (bf16[594,3584]{1,0:T(8,128)(2,1)S(1)}, bf16[594,3584]{1,0:T(8,128)(2,1)}, u32[]{:S(2)}) copy-start(bf16[594,3584]{1,0:T(8,128)(2,1)} %own_ref.1) | copy-start | bytes 12773380
  104.9 12.6 %all-to-all-start.1 = ((f32[4,2,96]{2,1,0:T(2,128)}), f32[4,2,96]{2,1,0:T(2,128)S(1)}, u32[]{:S(2)}, u32[]{:S(2)}) async-start(f32[4,2,96]{2,1,0:T(2,128)} %shard_stats.1), calls=%async_computation.1 | async-start | bytes 8192 | tf_op jit(solution)/shard_map/all_to_all | solution.py:154
  108.1 22.9 %collective-permute-start.3 = (f32[3,96]{1,0:T(4,128)S(1)}, f32[3,96]{1,0:T(4,128)S(1)}, u32[]{:S(2)}, u32[]{:S(2)}) collective-permute-start(f32[3,96]{1,0:T(4,128)S(1)} %pad_maximum_fusion.1), channel_id=1, source_target_pairs={{0,12},{4,0},{8,4},{12,8},{1,13},{5,1},{9,5},{13,9},{2,14},{6,2},{... | collective-permute-start | bytes 3464 | tf_op jit(solution)/shard_map/ppermute | solution.py:149
  112.5 18.5 %collective-permute-start.2 = (f32[3,96]{1,0:T(4,128)S(1)}, f32[3,96]{1,0:T(4,128)S(1)}, u32[]{:S(2)}, u32[]{:S(2)}) collective-permute-start(f32[3,96]{1,0:T(4,128)S(1)} %pad_maximum_fusion.1), channel_id=1, source_target_pairs={{0,8},{4,12},{8,0},{12,4},{1,9},{5,13},{9,1},{13,5},{2,10},{6,14},... | collective-permute-start | bytes 3464 | tf_op jit(solution)/shard_map/ppermute | solution.py:149
  114.9 16.1 %collective-permute-start.1 = (f32[3,96]{1,0:T(4,128)S(1)}, f32[3,96]{1,0:T(4,128)S(1)}, u32[]{:S(2)}, u32[]{:S(2)}) collective-permute-start(f32[3,96]{1,0:T(4,128)S(1)} %pad_maximum_fusion.1), channel_id=1, source_target_pairs={{0,4},{4,8},{8,12},{12,0},{1,5},{5,9},{9,13},{13,1},{2,6},{6,10},{... | collective-permute-start | bytes 3464 | tf_op jit(solution)/shard_map/ppermute | solution.py:149
  118.2 34.9 %all-to-all-start.2 = ((f32[32,2,96]{2,1,0:T(2,128)}), f32[32,2,96]{2,1,0:T(2,128)S(1)}, u32[]{:S(2)}, u32[]{:S(2)}) async-start(f32[32,2,96]{2,1,0:T(2,128)} %broadcast_in_dim.43), calls=%async_computation.2 | async-start | bytes 65536 | tf_op jit(solution)/shard_map/all_to_all | solution.py:26
  155.8 31.0 %all-to-all-start.3 = ((f32[32,1,2]{2,1,0:T(1,128)}), f32[32,1,2]{2,1,0:T(1,128)S(1)}, u32[]{:S(2)}, u32[]{:S(2)}) async-start(f32[32,1,2]{2,1,0:T(1,128)} %broadcast_in_dim.45), calls=%async_computation.3 | async-start | bytes 32768 | tf_op jit(solution)/shard_map/all_to_all | solution.py:26

commit v3 on v2

v3 whole, which is shorter than its diff:
```python
import jax
import jax.numpy as jnp
from jax import lax
from jax.experimental import pallas as pl
from jax.experimental.pallas import tpu as pltpu
from jax.sharding import Mesh
from jax.sharding import PartitionSpec as P


Z = ("zh", "zl")
ROW = ("zh", "zl", "c", "y")
PROMPT = ("zh", "zl", "c")
PLANE = ("c", "x", "y")
LANES = 128
FIELDS = 6
FULL_VMEM = 60 * 1024 * 2**10
KERNEL_VMEM = 48 * 2**20
SMALL_VMEM = 4 * 2**20

clip_low = 0.8
clip_high = 1.2
dual_clip = 3.0
kl_weight = 0.04
reward_unit = 0.01
std_floor = 0.5


def from_everyone(array, axis):
    devices = lax.axis_size(axis)
    return lax.all_to_all(
        jnp.broadcast_to(array[None], (devices, *array.shape)), axis, 0, 0, tiled=True
    )


def prep_kernel(y_ref, *refs):
    smalls, hidden_ref, out_ref, tall_ref = refs[:7], refs[7], refs[8], refs[9]
    landed, sems = refs[10:17], refs[17]
    copies = [
        pltpu.make_async_copy(src, dst, sems.at[i])
        for i, (src, dst) in enumerate(zip(smalls, landed))
    ]
    for copy in copies:
        copy.start()
    for copy in copies:
        copy.wait()
    ids_ref, old_ref, ref_ref, mask_ref, len_ref, valid_ref, reward_ref = landed
    local_rows, width = hidden_ref.shape[1:]
    blocks = width // LANES
    lane = lax.broadcasted_iota(jnp.int32, (local_rows, LANES), 1)
    line = lax.broadcasted_iota(jnp.int32, (local_rows, LANES), 0)
    field = lane // 3
    values = jnp.zeros((local_rows, LANES), jnp.float32)
    for r in range(local_rows):
        position = y_ref[0] * local_rows + r
        live = (mask_ref[0, r] == 1) & (position < len_ref[0]) & (valid_ref[0] == 1)
        whole = jnp.where(
            field == 0,
            ids_ref[0, r],
            jnp.where(
                field == 3,
                live.astype(jnp.int32),
                jnp.where(
                    field == 4, valid_ref[0], jnp.where(field == 5, reward_ref[0], 0)
                ),
            ),
        ).astype(jnp.float32)
        row = jnp.where(
            field == 1, old_ref[0, r], jnp.where(field == 2, ref_ref[0, r], whole)
        )
        values = jnp.where(line == r, row, values)
    first = values.astype(jnp.bfloat16).astype(jnp.float32)
    rest = values - first
    second = rest.astype(jnp.bfloat16).astype(jnp.float32)
    piece = lane - 3 * field
    side = jnp.where(piece == 0, first, jnp.where(piece == 1, second, rest - second))
    tall_ref[...] = jnp.zeros(tall_ref.shape, jnp.float32)
    for r in range(local_rows):
        at = r * (blocks + 1)
        for j in range(blocks):
            part = hidden_ref[0, r : r + 1, j * LANES : (j + 1) * LANES]
            tall_ref[at + j : at + j + 1, :] = part.astype(jnp.float32)
        tall_ref[at + blocks : at + blocks + 1, :] = side[r : r + 1, :]
    out_ref[...] = tall_ref[...].astype(jnp.bfloat16)


def prepared(y, smalls, hidden):
    _, local_rows, width = hidden.shape
    tall = -(-local_rows * (width // LANES + 1) // 8) * 8
    vmem = pl.BlockSpec(memory_space=pltpu.VMEM)
    return pl.pallas_call(
        prep_kernel,
        in_specs=[pl.BlockSpec(memory_space=pltpu.SMEM)]
        + [pl.BlockSpec(memory_space=pltpu.HBM)] * len(smalls)
        + [vmem],
        out_specs=vmem,
        out_shape=jax.ShapeDtypeStruct((tall, LANES), jnp.bfloat16),
        scratch_shapes=[
            pltpu.VMEM((tall, LANES), jnp.float32),
            *(pltpu.SMEM(small.shape, small.dtype) for small in smalls),
            pltpu.SemaphoreType.DMA((len(smalls),)),
        ],
        compiler_params=pltpu.CompilerParams(vmem_limit_bytes=FULL_VMEM),
        name="prep",
    )(y, *smalls, hidden)


def tail_kernel(back_ref, side_ref, adv_ref, logp_ref, loss_ref, totals_ref):
    lse = back_ref[:, 0, :]
    peak = jnp.max(lse, axis=0, keepdims=True)
    total = jnp.sum(jnp.exp(lse - peak), axis=0, keepdims=True)
    target = jnp.sum(back_ref[:, 1, :], axis=0, keepdims=True)
    raw_logp = target - (peak + jnp.log(total))
    live_float = side_ref[3:4, :]
    live = live_float > 0.5
    adv_rows = adv_ref[...]
    prob_ratio = jnp.exp(raw_logp - side_ref[1:2, :])
    gain_side = adv_rows * jnp.minimum(prob_ratio, clip_high)
    loss_side = jnp.maximum(adv_rows * jnp.maximum(prob_ratio, clip_low), dual_clip * adv_rows)
    objective = jnp.where(adv_rows >= 0.0, gain_side, loss_side)
    log_gap = side_ref[2:3, :] - raw_logp
    kl_term = jnp.exp(log_gap) - log_gap - 1.0
    token_loss = jnp.where(live, kl_weight * kl_term - objective, 0.0)
    logp_ref[...] = jnp.where(live, raw_logp, 0.0)
    loss_ref[...] = token_loss
    lane = lax.broadcasted_iota(jnp.int32, totals_ref.shape, 2)
    totals_ref[...] = jnp.where(
        lane == 0, jnp.sum(token_loss), jnp.where(lane == 1, jnp.sum(live_float), 0.0)
    )


def finished(back, side, adv_rows, devices):
    row = jax.ShapeDtypeStruct(adv_rows.shape, jnp.float32)
    vmem = pl.BlockSpec(memory_space=pltpu.VMEM)
    return pl.pallas_call(
        tail_kernel,
        in_specs=[vmem] * 3,
        out_specs=[vmem] * 3,
        out_shape=[row, row, jax.ShapeDtypeStruct((devices, 1, LANES), jnp.float32)],
        compiler_params=pltpu.CompilerParams(vmem_limit_bytes=SMALL_VMEM),
        name="tail",
    )(back, side, adv_rows)


def stats_kernel(start_ref, x_ref, own_ref, other_ref, out_ref, weights_ref, sems):
    groups, _, per = out_ref.shape
    vocab, width = own_ref.shape
    half = 8 * LANES
    copies = [
        pltpu.make_async_copy(own_ref.at[:, :half], weights_ref.at[0, :, :half], sems.at[0]),
        pltpu.make_async_copy(own_ref.at[:, half:], weights_ref.at[0, :, half:], sems.at[1]),
        pltpu.make_async_copy(other_ref, weights_ref.at[1], sems.at[2]),
    ]
    for copy in copies:
        copy.start()
    contract = (((1,), (1,)), ((), ()))

    def product(left, right):
        return lax.dot_general(left, right, contract, preferred_element_type=jnp.float32)

    pick = (lax.broadcasted_iota(jnp.int32, (8, LANES), 1) < 3).astype(jnp.bfloat16)
    ids = product(pick, x_ref[:, width:])[0:1].astype(jnp.int32)
    line = lax.broadcasted_iota(jnp.int32, (vocab, x_ref.shape[0]), 0)

    def stats(logits, start):
        peak = jnp.max(logits, axis=0, keepdims=True)
        total = jnp.sum(jnp.exp(logits - peak), axis=0, keepdims=True)
        hit = line == ids - start
        return peak, total, jnp.sum(jnp.where(hit, logits, 0.0), axis=0, keepdims=True)

    copies[0].wait()
    logits = product(weights_ref[0, :, :half], x_ref[:, :half])
    copies[1].wait()
    logits += product(weights_ref[0, :, half:], x_ref[:, half:width])
    peak_a, total_a, target_a = stats(logits, start_ref[0])
    copies[2].wait()
    logits = product(weights_ref[1], x_ref[:, :width])
    peak_b, total_b, target_b = stats(logits, start_ref[1])
    peak = jnp.maximum(peak_a, peak_b)
    total = total_a * jnp.exp(peak_a - peak) + total_b * jnp.exp(peak_b - peak)
    lse = peak + jnp.log(total)
    target = target_a + target_b
    for g in range(groups):
        out_ref[g, 0:1, :] = lse[:, g * per : (g + 1) * per]
        out_ref[g, 1:2, :] = target[:, g * per : (g + 1) * per]


def shard_stats(rows, own, other, starts, groups):
    count = rows.shape[0]
    vocab, width = own.shape
    return pl.pallas_call(
        stats_kernel,
        in_specs=[
            pl.BlockSpec(memory_space=pltpu.SMEM),
            pl.BlockSpec(memory_space=pltpu.VMEM),
            pl.BlockSpec(memory_space=pltpu.HBM),
            pl.BlockSpec(memory_space=pltpu.HBM),
        ],
        out_specs=pl.BlockSpec(memory_space=pltpu.VMEM),
        out_shape=jax.ShapeDtypeStruct((groups, 2, count // groups), jnp.float32),
        scratch_shapes=[
            pltpu.VMEM((2, vocab, width), jnp.bfloat16),
            pltpu.SemaphoreType.DMA((3,)),
        ],
        cost_estimate=pl.CostEstimate(
            flops=4 * count * width * vocab,
            bytes_accessed=2 * width * (count + 2 * vocab),
            transcendentals=2 * count * vocab,
        ),
        compiler_params=pltpu.CompilerParams(vmem_limit_bytes=KERNEL_VMEM),
        name="shard_stats",
    )(starts, rows, own, other)


def merged(lse):
    peak = jnp.max(lse, axis=0)
    return peak + jnp.log(jnp.sum(jnp.exp(lse - peak), axis=0))


def group_advantages(sums, valid_f, scores):
    group_count, first_moment, second_moment = (sums[i : i + 1] for i in range(3))
    safe_count = jnp.maximum(group_count, 1.0)
    group_mean = first_moment / safe_count
    spread = jnp.sqrt(jnp.maximum(second_moment / safe_count - group_mean * group_mean, 0.0))
    return valid_f * (scores - group_mean) / jnp.maximum(spread, std_floor)


def local(
    hidden, unembed, token_ids, old_logp, ref_logp, loss_mask, lengths, sample_valid, rewards
):
    _, local_rows, width = hidden.shape
    vocab_rows = unembed.shape[0]
    n_x = lax.axis_size("x")
    n_y = lax.axis_size("y")
    n_z = lax.axis_size(Z)
    column_rows = n_z * local_rows
    core = lax.axis_index("c")

    full = width + LANES
    y = lax.axis_index("y")
    singles = (lengths.reshape(1), sample_valid.reshape(1), rewards.reshape(1))
    smalls = (token_ids, old_logp, ref_logp, loss_mask, *singles)
    chunk = prepared(y.reshape(1), smalls, hidden)
    column = lax.all_gather(lax.all_gather(chunk, "zh", axis=0), "zl", axis=0)
    column = column.reshape(n_z, *chunk.shape)
    rows = column[:, : local_rows * full // LANES].reshape(column_rows, full)

    other_unembed = lax.ppermute(unembed, "c", [(0, 1), (1, 0)])
    gathered = from_everyone(rows, "y").reshape(n_y * column_rows, full)

    side = rows[:, width : width + 3 * FIELDS].astype(jnp.float32).T
    side = side.reshape(FIELDS, 3, column_rows)
    side = side[:, 0] + side[:, 1] + side[:, 2]
    valid_f = side[4:5]
    scores = side[5:6] * reward_unit
    moments = jnp.concatenate([valid_f, valid_f * scores, valid_f * scores * scores])
    terms = [moments]
    for d in range(1, n_x):
        ring = [(i, (i + d) % n_x) for i in range(n_x)]
        terms.append(lax.ppermute(moments, "x", ring))
    adv_rows = group_advantages(sum(terms), valid_f, scores)
    z = lax.axis_index(Z)
    shards = jnp.stack([(z * 2 + core) * n_y, (z * 2 + 1 - core) * n_y]) + y
    stats = shard_stats(gathered, unembed, other_unembed, shards * vocab_rows, n_y)
    plane = lax.all_to_all(stats, "y", 0, 0, tiled=True)
    plane = jnp.concatenate([merged(plane[:, 0:1]), jnp.sum(plane[:, 1:2], axis=0)])
    back = from_everyone(plane, Z)
    n_plane = lax.axis_size(PLANE)
    token_logp, token_loss, totals = finished(back, side, adv_rows, n_plane)
    totals = jnp.sum(lax.all_to_all(totals, PLANE, 0, 0, tiled=True), axis=(0, 1))
    loss = totals[0] / jnp.maximum(totals[1], 1.0)
    place = lax.axis_index("zl") * lax.axis_size("zh") + lax.axis_index("zh")
    first = place * local_rows
    return (
        lax.dynamic_slice_in_dim(token_logp, first, local_rows, 1),
        lax.dynamic_slice_in_dim(token_loss, first, local_rows, 1),
        lax.dynamic_slice_in_dim(adv_rows, first, 1, 1),
        loss,
    )


def solution(mesh):
    split = Mesh(
        mesh.devices.reshape(
            mesh.shape["prompt"] // 4, 2, 2, mesh.shape["sample"], mesh.shape["vocab"]
        ),
        ("zh", "zl", "c", "x", "y"),
    )
    in_specs = (
        P("x", ROW, None),
        P(ROW, None),
        P("x", ROW),
        P("x", ROW),
        P("x", ROW),
        P("x", ROW),
        P(PROMPT, "x"),
        P(PROMPT, "x"),
        P(PROMPT, "x"),
    )
    out_specs = (P("x", ROW), P("x", ROW), P(PROMPT, "x"), P())
    return jax.shard_map(local, mesh=split, in_specs=in_specs, out_specs=out_specs, check_vma=False)
```

time: 191 us -> 171 us (0.90)
  blocking collectives: 45.7 us -> 38 us
  starting transfers between devices: 69.7 us -> 63.3 us
  other arithmetic: 5.77 us -> 1 us
  local copies, waits for them, and re-layouts: 9.17 us -> 5.07 us
  Pallas kernels: 7.85 us -> 11.6 us
    all_to_all x3 -> x2, starting transfers between devices: 41.1 us -> 18.2 us  [from_everyone(): lax.all_to_all(jnp.broadcast_to(array[None], (devices, *array.shape)), ax...]
    all_to_all x0 -> x1, starting transfers between devices: none -> 16 us  [local(): lax.all_to_all(totals, PLANE, 0, 0, tiled=True)]
    all_to_all x3 -> x2, waiting for transfers between devices: 46.4 us -> 35.7 us  [from_everyone(): lax.all_to_all(jnp.broadcast_to(array[None], (devices, *array.shape)), ax...]
    all_gather x1 -> x2, blocking collectives: 45.7 us -> 38 us  [local(): column = lax.all_gather(lax.all_gather(chunk, 'zh', axis=0), 'zl', axis=0)]
    all_to_all x0 -> x1, waiting for transfers between devices: none -> 6.14 us  [local(): lax.all_to_all(totals, PLANE, 0, 0, tiled=True)]
    all_to_all x1, waiting for transfers between devices: 0.01 us -> 4.05 us  [local(): plane = lax.all_to_all(stats, 'y', 0, 0, tiled=True)]
    pallas_call x0 -> x2, Pallas kernels: none -> 2.95 us  [the longest x1 2.17 us: prepared(): pl.pallas_call(prep_kernel, in_specs=[pl.BlockSpec(memory_space=pltpu.SME...]
    unnamed x4 -> x2, local copies, waits for them, and re-layouts: 2.22 us -> 0.01 us
  transfers between devices with their start and end apart: 8 -> 8, of which waited for: 3 -> 4; matrix products, arithmetic and copies ran while one was open for 5% -> 3% of each run, Pallas kernels for 0% -> 6%
where the time goes in v3:
time: 171 us; the launch traced here: 170 us
  starting transfers between devices  63.3 us (37%)
  waiting for transfers between devices  45.9 us (27%)
  blocking collectives  38 us (22%)
  Pallas kernels  11.6 us (7%)
  between operations  5.09 us (3%)
  local copies, waits for them, and re-layouts  5.07 us (3%)
    all_gather x2, blocking collectives, local(): column = lax.all_gather(lax.all_gather(chunk, 'zh', axis=0), 'zl', axis=0)  38 us
    all_to_all x2, waiting for transfers between devices, from_everyone(): lax.all_to_all(jnp.broadcast_to(array[None], (devices, *array.shape)), ax...  35.7 us
    all_to_all x2, starting transfers between devices, from_everyone(): lax.all_to_all(jnp.broadcast_to(array[None], (devices, *array.shape)), ax...  18.2 us
    ppermute x1, starting transfers between devices, local(): other_unembed = lax.ppermute(unembed, 'c', [(0, 1), (1, 0)])  16 us
    all_to_all x1, starting transfers between devices, local(): lax.all_to_all(totals, PLANE, 0, 0, tiled=True)  16 us
    ppermute x3, starting transfers between devices, local(): terms.append(lax.ppermute(moments, 'x', ring))  9.93 us
    pallas_call x1, Pallas kernels, shard_stats(): pl.pallas_call(stats_kernel, in_specs=[pl.BlockSpec(memory_space=pltpu.SM...  8.69 us
    all_to_all x1, waiting for transfers between devices, local(): lax.all_to_all(totals, PLANE, 0, 0, tiled=True)  6.14 us
  transfers between devices with their start and end apart: 8, of which 4 were waited for; matrix products, arithmetic and copies ran while one was open for 3% of the time, Pallas kernels for 6%

profile of v3, /device:TPU:1, one launch (start us, length us, event | category | flops | bytes accessed | tf_op | source)
XLA Modules:
  0.0 170.0 jit_solution(4582394897841480816)
XLA Ops:
  0.6 16.0 %collective-permute-start = (bf16[594,3584]{1,0:T(8,128)(2,1)}, bf16[594,3584]{1,0:T(8,128)(2,1)}, u32[]{:S(2)}, u32[]{:S(2)}) collective-permute-start(bf16[594,3584]{1,0:T(8,128)(2,1)} %own_ref.1), channel_id=1, source_target_pairs={{0,16},{16,0},{1,17},{17,1},{2,18},{18,2},{3,19},{19,3},{4,20},{20... | collective-permute-start | bytes 12773384 | tf_op jit(solution)/shard_map/ppermute | solution.py:247
  18.6 2.2 %prep.1 = bf16[88,128]{1,0:T(8,128)(2,1)} custom-call(s32[1]{0:T(128)} %bitcast.2.y_ref, s32[1,3]{1,0:T(1,128)} %refs_0_.1, f32[1,3]{1,0:T(1,128)} %refs_1_.1, f32[1,3]{1,0:T(1,128)} %refs_2_.1, s32[1,3]{1,0:T(1,128)} %refs_3_.1, s32[1]{0:T(128)} %bitcast.34.refs_4_, s32[1]{0:T(128)} %bitcast.35.refs_5_, s32[1]{0:T(128)} %bitcast.36.refs_6_, ...), custom_call_target="tpu_custom_call" | custom-call | tf_op jit(solution)/shard_map/prep/pallas_call | solution.py:90
  20.8 30.6 %all-gather = bf16[1408,128]{1,0:T(8,128)(2,1)S(1)} all-gather(bf16[88,128]{1,0:T(8,128)(2,1)} %prep.1), channel_id=2, replica_groups=mesh['zh'=16,'zl'=2,'c'=2,'x'=4,'y'=4] {'zh'}, dimensions={0}, use_global_device_ids=true | all-gather | bytes 382976 | tf_op jit(solution)/shard_map/all_gather | solution.py:243
  51.4 7.4 %all-gather.1 = bf16[32,88,128]{2,1,0:T(8,128)(2,1)S(1)} all-gather(bf16[16,88,128]{2,1,0:T(8,128)(2,1)S(1)} %bitcast.40), channel_id=3, replica_groups=mesh['zh'=16,'zl'=2,'c'=2,'x'=4,'y'=4] {'zl'}, dimensions={0}, use_global_device_ids=true | all-gather | bytes 1081344 | tf_op jit(solution)/shard_map/all_gather | solution.py:243
  58.8 0.8 broadcast_in_dim.6
  59.6 1.8 %broadcast_in_dim.7 = bf16[4,96,3712]{2,1,0:T(8,128)(2,1)} broadcast(bf16[96,3712]{1,0:T(8,128)(2,1)S(1)} %broadcast_in_dim.6), dimensions={1,2} | broadcast | bytes 3563520 | tf_op jit(solution)/shard_map/broadcast_in_dim | solution.py:31
  61.4 4.2 %all-to-all-start = ((bf16[4,96,3712]{2,1,0:T(8,128)(2,1)}), bf16[4,96,3712]{2,1,0:T(8,128)(2,1)S(1)}, u32[]{:S(2)}, u32[]{:S(2)}) async-start(bf16[4,96,3712]{2,1,0:T(8,128)(2,1)} %broadcast_in_dim.7), calls=%async_computation | async-start | bytes 5701632 | tf_op jit(solution)/shard_map/all_to_all | solution.py:30
  65.6 0.7 convert_bitcast_fusion
  66.5 4.7 %collective-permute-start.2 = (f32[3,96]{1,0:T(4,128)S(1)}, f32[3,96]{1,0:T(4,128)S(1)}, u32[]{:S(2)}, u32[]{:S(2)}) collective-permute-start(f32[3,96]{1,0:T(4,128)S(1)} %pad_maximum_fusion), channel_id=1, source_target_pairs={{0,8},{4,12},{8,0},{12,4},{1,9},{5,13},{9,1},{13,5},{2,10},{6,14},... | collective-permute-start | bytes 3464 | tf_op jit(solution)/shard_map/ppermute | solution.py:259
  71.2 2.8 %collective-permute-start.3 = (f32[3,96]{1,0:T(4,128)S(1)}, f32[3,96]{1,0:T(4,128)S(1)}, u32[]{:S(2)}, u32[]{:S(2)}) collective-permute-start(f32[3,96]{1,0:T(4,128)S(1)} %pad_maximum_fusion), channel_id=1, source_target_pairs={{0,12},{4,0},{8,4},{12,8},{1,13},{5,1},{9,5},{13,9},{2,14},{6,2},{... | collective-permute-start | bytes 3464 | tf_op jit(solution)/shard_map/ppermute | solution.py:259
  73.9 2.5 %collective-permute-start.1 = (f32[3,96]{1,0:T(4,128)S(1)}, f32[3,96]{1,0:T(4,128)S(1)}, u32[]{:S(2)}, u32[]{:S(2)}) collective-permute-start(f32[3,96]{1,0:T(4,128)S(1)} %pad_maximum_fusion), channel_id=1, source_target_pairs={{0,4},{4,8},{8,12},{12,0},{1,5},{5,9},{9,13},{13,1},{2,6},{6,10},{... | collective-permute-start | bytes 3464 | tf_op jit(solution)/shard_map/ppermute | solution.py:259
  76.5 14.3 %all-to-all-done = bf16[4,96,3712]{2,1,0:T(8,128)(2,1)S(1)} async-done(((bf16[4,96,3712]{2,1,0:T(8,128)(2,1)}), bf16[4,96,3712]{2,1,0:T(8,128)(2,1)S(1)}, u32[]{:S(2)}, u32[]{:S(2)}) %all-to-all-start) | async-done | bytes 2850848 | tf_op jit(solution)/shard_map/all_to_all | solution.py:30
  90.8 8.7 %shard_stats.1 = f32[4,2,96]{2,1,0:T(2,128)} custom-call(s32[2]{0:T(128)S(1)} %fusion.start_ref, bf16[384,3712]{1,0:T(8,128)(2,1)S(1)} %bitcast.37, bf16[594,3584]{1,0:T(8,128)(2,1)} %own_ref.1, bf16[594,3584]{1,0:T(8,128)(2,1)} %collective-permute-done.other_ref), custom_call_target="tpu_custom_call" | custom-call | flops 3269984256 | bytes 11268096 | tf_op jit(solution)/shard_map/shard_stats/pallas_call | solution.py:190
  99.5 3.2 %all-to-all-start.1 = ((f32[4,2,96]{2,1,0:T(2,128)}), f32[4,2,96]{2,1,0:T(2,128)S(1)}, u32[]{:S(2)}, u32[]{:S(2)}) async-start(f32[4,2,96]{2,1,0:T(2,128)} %shard_stats.1), calls=%async_computation.1 | async-start | bytes 8192 | tf_op jit(solution)/shard_map/all_to_all | solution.py:264
  102.8 4.0 %all-to-all-done.1 = f32[4,2,96]{2,1,0:T(2,128)S(1)} async-done(((f32[4,2,96]{2,1,0:T(2,128)}), f32[4,2,96]{2,1,0:T(2,128)S(1)}, u32[]{:S(2)}, u32[]{:S(2)}) %all-to-all-start.1) | async-done | bytes 3104 | tf_op jit(solution)/shard_map/all_to_all | solution.py:264
  107.0 0.6 broadcast_in_dim.16
  107.6 14.0 %all-to-all-start.2 = ((f32[32,2,96]{2,1,0:T(2,128)}), f32[32,2,96]{2,1,0:T(2,128)S(1)}, u32[]{:S(2)}, u32[]{:S(2)}) async-start(f32[32,2,96]{2,1,0:T(2,128)} %broadcast_in_dim.16), calls=%async_computation.2 | async-start | bytes 65536 | tf_op jit(solution)/shard_map/all_to_all | solution.py:30
  121.6 0.6 constant_dynamic-slice_fusion
  122.2 21.4 %all-to-all-done.2.back_ref = f32[32,2,96]{2,1,0:T(2,128)S(1)} async-done(((f32[32,2,96]{2,1,0:T(2,128)}), f32[32,2,96]{2,1,0:T(2,128)S(1)}, u32[]{:S(2)}, u32[]{:S(2)}) %all-to-all-start.2) | async-done | bytes 24608 | tf_op jit(solution)/shard_map/all_to_all | solution.py:30
  143.6 0.8 tail.1
  144.3 16.0 %all-to-all-start.3 = ((f32[32,1,128]{2,1,0:T(1,128)}), f32[32,1,128]{2,1,0:T(1,128)S(1)}, u32[]{:S(2)}, u32[]{:S(2)}) async-start(f32[32,1,128]{2,1,0:T(1,128)} %get-tuple-element.9), calls=%async_computation.3 | async-start | bytes 32768 | tf_op jit(solution)/shard_map/all_to_all | solution.py:269
  160.3 0.6 constant_dynamic-slice_fusion.1
  160.9 6.1 %all-to-all-done.3 = f32[32,1,128]{2,1,0:T(1,128)S(1)} async-done(((f32[32,1,128]{2,1,0:T(1,128)}), f32[32,1,128]{2,1,0:T(1,128)S(1)}, u32[]{:S(2)}, u32[]{:S(2)}) %all-to-all-start.3) | async-done | bytes 16416 | tf_op jit(solution)/shard_map/all_to_all | solution.py:269
  167.1 0.6 fusion.4
  (21 shorter events, 0.4 us)
Async XLA Ops:
  0.6 90.2 %collective-permute-start = (bf16[594,3584]{1,0:T(8,128)(2,1)}, bf16[594,3584]{1,0:T(8,128)(2,1)}, u32[]{:S(2)}, u32[]{:S(2)}) collective-permute-start(bf16[594,3584]{1,0:T(8,128)(2,1)} %own_ref.1), channel_id=1, source_target_pairs={{0,16},{16,0},{1,17},{17,1},{2,18},{18,2},{3,19},{19,3},{4,20},{20... | collective-permute-start | bytes 12773384 | tf_op jit(solution)/shard_map/ppermute | solution.py:247
  59.6 1.8 %copy-start = (bf16[96,3712]{1,0:T(8,128)(2,1)}, bf16[96,3712]{1,0:T(8,128)(2,1)S(1)}, u32[]{:S(2)}) copy-start(bf16[96,3712]{1,0:T(8,128)(2,1)S(1)} %broadcast_in_dim.6) | copy-start | bytes 2138116
  61.4 29.4 %all-to-all-start = ((bf16[4,96,3712]{2,1,0:T(8,128)(2,1)}), bf16[4,96,3712]{2,1,0:T(8,128)(2,1)S(1)}, u32[]{:S(2)}, u32[]{:S(2)}) async-start(bf16[4,96,3712]{2,1,0:T(8,128)(2,1)} %broadcast_in_dim.7), calls=%async_computation | async-start | bytes 5701632 | tf_op jit(solution)/shard_map/all_to_all | solution.py:30
  66.5 36.3 %collective-permute-start.2 = (f32[3,96]{1,0:T(4,128)S(1)}, f32[3,96]{1,0:T(4,128)S(1)}, u32[]{:S(2)}, u32[]{:S(2)}) collective-permute-start(f32[3,96]{1,0:T(4,128)S(1)} %pad_maximum_fusion), channel_id=1, source_target_pairs={{0,8},{4,12},{8,0},{12,4},{1,9},{5,13},{9,1},{13,5},{2,10},{6,14},... | collective-permute-start | bytes 3464 | tf_op jit(solution)/shard_map/ppermute | solution.py:259
  71.2 31.6 %collective-permute-start.3 = (f32[3,96]{1,0:T(4,128)S(1)}, f32[3,96]{1,0:T(4,128)S(1)}, u32[]{:S(2)}, u32[]{:S(2)}) collective-permute-start(f32[3,96]{1,0:T(4,128)S(1)} %pad_maximum_fusion), channel_id=1, source_target_pairs={{0,12},{4,0},{8,4},{12,8},{1,13},{5,1},{9,5},{13,9},{2,14},{6,2},{... | collective-permute-start | bytes 3464 | tf_op jit(solution)/shard_map/ppermute | solution.py:259
  73.9 28.9 %collective-permute-start.1 = (f32[3,96]{1,0:T(4,128)S(1)}, f32[3,96]{1,0:T(4,128)S(1)}, u32[]{:S(2)}, u32[]{:S(2)}) collective-permute-start(f32[3,96]{1,0:T(4,128)S(1)} %pad_maximum_fusion), channel_id=1, source_target_pairs={{0,4},{4,8},{8,12},{12,0},{1,5},{5,9},{9,13},{13,1},{2,6},{6,10},{... | collective-permute-start | bytes 3464 | tf_op jit(solution)/shard_map/ppermute | solution.py:259
  99.5 7.3 %all-to-all-start.1 = ((f32[4,2,96]{2,1,0:T(2,128)}), f32[4,2,96]{2,1,0:T(2,128)S(1)}, u32[]{:S(2)}, u32[]{:S(2)}) async-start(f32[4,2,96]{2,1,0:T(2,128)} %shard_stats.1), calls=%async_computation.1 | async-start | bytes 8192 | tf_op jit(solution)/shard_map/all_to_all | solution.py:264
  107.6 36.0 %all-to-all-start.2 = ((f32[32,2,96]{2,1,0:T(2,128)}), f32[32,2,96]{2,1,0:T(2,128)S(1)}, u32[]{:S(2)}, u32[]{:S(2)}) async-start(f32[32,2,96]{2,1,0:T(2,128)} %broadcast_in_dim.16), calls=%async_computation.2 | async-start | bytes 65536 | tf_op jit(solution)/shard_map/all_to_all | solution.py:30
  144.3 22.7 %all-to-all-start.3 = ((f32[32,1,128]{2,1,0:T(1,128)}), f32[32,1,128]{2,1,0:T(1,128)S(1)}, u32[]{:S(2)}, u32[]{:S(2)}) async-start(f32[32,1,128]{2,1,0:T(1,128)} %get-tuple-element.9), calls=%async_computation.3 | async-start | bytes 32768 | tf_op jit(solution)/shard_map/all_to_all | solution.py:269

commit v4 on v3

--- a/solution.py
+++ b/solution.py
@@ -15,6 +15,7 @@
 FIELDS = 6
 FULL_VMEM = 60 * 1024 * 2**10
 KERNEL_VMEM = 48 * 2**20
+LATE_VMEM = 24 * 2**20
 SMALL_VMEM = 4 * 2**20
 
 clip_low = 0.8
@@ -141,74 +142,116 @@
     )(back, side, adv_rows)
 
 
-def stats_kernel(start_ref, x_ref, own_ref, other_ref, out_ref, weights_ref, sems):
-    groups, _, per = out_ref.shape
-    vocab, width = own_ref.shape
-    half = 8 * LANES
+CONTRACT = (((1,), (1,)), ((), ()))
+FIRST = 64
+
+
+def product(left, right):
+    return lax.dot_general(left, right, CONTRACT, preferred_element_type=jnp.float32)
+
+
+def row_ids(x_ref, width):
+    pick = (lax.broadcasted_iota(jnp.int32, (8, LANES), 1) < 3).astype(jnp.bfloat16)
+    return product(pick, x_ref[:, width:])[0:1].astype(jnp.int32)
+
+
+def half_stats(logits, ids):
+    peak = jnp.max(logits, axis=0, keepdims=True)
+    total = jnp.sum(jnp.exp(logits - peak), axis=0, keepdims=True)
+    hit = lax.broadcasted_iota(jnp.int32, logits.shape, 0) == ids
+    return peak, total, jnp.sum(jnp.where(hit, logits, 0.0), axis=0, keepdims=True)
+
+
+def joined(first, second):
+    (peak_a, total_a, target_a), (peak_b, total_b, target_b) = first, second
+    peak = jnp.maximum(peak_a, peak_b)
+    total = total_a * jnp.exp(peak_a - peak) + total_b * jnp.exp(peak_b - peak)
+    return jnp.concatenate([peak + jnp.log(total), target_a + target_b])
+
+
+def early_kernel(
+    scalars_ref, own_ref, other_ref, rows_ref, above_ref, below_ref, out_ref, x_ref, w_ref, sems
+):
+    per = out_ref.shape[2]
+    width = own_ref.shape[1]
+    cut = 8 * LANES
     copies = [
-        pltpu.make_async_copy(own_ref.at[:, :half], weights_ref.at[0, :, :half], sems.at[0]),
-        pltpu.make_async_copy(own_ref.at[:, half:], weights_ref.at[0, :, half:], sems.at[1]),
-        pltpu.make_async_copy(other_ref, weights_ref.at[1], sems.at[2]),
+        pltpu.make_async_copy(own_ref.at[:, :cut], w_ref.at[0, :, :cut], sems.at[0]),
+        pltpu.make_async_copy(own_ref.at[:, cut:], w_ref.at[0, :, cut:], sems.at[1]),
+        pltpu.make_async_copy(other_ref, w_ref.at[1], sems.at[2]),
     ]
     for copy in copies:
         copy.start()
-    contract = (((1,), (1,)), ((), ()))
-
-    def product(left, right):
-        return lax.dot_general(left, right, contract, preferred_element_type=jnp.float32)
-
-    pick = (lax.broadcasted_iota(jnp.int32, (8, LANES), 1) < 3).astype(jnp.bfloat16)
-    ids = product(pick, x_ref[:, width:])[0:1].astype(jnp.int32)
-    line = lax.broadcasted_iota(jnp.int32, (vocab, x_ref.shape[0]), 0)
-
-    def stats(logits, start):
-        peak = jnp.max(logits, axis=0, keepdims=True)
-        total = jnp.sum(jnp.exp(logits - peak), axis=0, keepdims=True)
-        hit = line == ids - start
-        return peak, total, jnp.sum(jnp.where(hit, logits, 0.0), axis=0, keepdims=True)
-
+    x_ref[:per, :] = rows_ref[...]
+    x_ref[per : 2 * per, :] = above_ref[...]
+    x_ref[2 * per :, :] = below_ref[:FIRST, :]
+    ids = row_ids(x_ref, width)
     copies[0].wait()
-    logits = product(weights_ref[0, :, :half], x_ref[:, :half])
+    logits = product(w_ref[0, :, :cut], x_ref[:, :cut])
     copies[1].wait()
-    logits += product(weights_ref[0, :, half:], x_ref[:, half:width])
-    peak_a, total_a, target_a = stats(logits, start_ref[0])
+    logits += product(w_ref[0, :, cut:], x_ref[:, cut:width])
+    first = half_stats(logits, ids - scalars_ref[0])
     copies[2].wait()
-    logits = product(weights_ref[1], x_ref[:, :width])
-    peak_b, total_b, target_b = stats(logits, start_ref[1])
-    peak = jnp.maximum(peak_a, peak_b)
-    total = total_a * jnp.exp(peak_a - peak) + total_b * jnp.exp(peak_b - peak)
-    lse = peak + jnp.log(total)
-    target = target_a + target_b
-    for g in range(groups):
-        out_ref[g, 0:1, :] = lse[:, g * per : (g + 1) * per]
-        out_ref[g, 1:2, :] = target[:, g * per : (g + 1) * per]
-
-
-def shard_stats(rows, own, other, starts, groups):
-    count = rows.shape[0]
+    logits = product(w_ref[1], x_ref[:, :width])
+    stats = joined(first, half_stats(logits, ids - scalars_ref[1]))
+    out_ref[0] = stats[:, :per]
+    out_ref[1] = stats[:, per : 2 * per]
+    out_ref[2] = jnp.concatenate(
+        [stats[:, 2 * per :], jnp.zeros((2, per - FIRST), jnp.float32)], axis=1
+    )
+
+
+def late_kernel(
+    scalars_ref, own_ref, other_ref, below_ref, low_ref, high_ref, early_ref, out_ref, x_ref
+):
+    per = out_ref.shape[2]
+    width = own_ref.shape[1]
+    rest = per - FIRST
+    half = per // 2
+    x_ref[:rest, :] = below_ref[FIRST:, :]
+    x_ref[rest : rest + half, :] = low_ref[...]
+    x_ref[rest + half :, :] = high_ref[...]
+    ids = row_ids(x_ref, width)
+    first = half_stats(product(own_ref[...], x_ref[:, :width]), ids - scalars_ref[0])
+    second = half_stats(product(other_ref[...], x_ref[:, :width]), ids - scalars_ref[1])
+    stats = joined(first, second)
+    y = scalars_ref[2]
+    out_ref[y] = early_ref[0]
+    out_ref[lax.rem(y + 1, 4)] = early_ref[1]
+    out_ref[lax.rem(y + 3, 4)] = jnp.concatenate(
+        [early_ref[2][:, :FIRST], stats[:, :rest]], axis=1
+    )
+    out_ref[lax.rem(y + 2, 4)] = stats[:, rest:]
+
+
+def shard_stats(kernel, scalars, own, other, operands, groups, count, staged):
     vocab, width = own.shape
-    return pl.pallas_call(
-        stats_kernel,
-        in_specs=[
-            pl.BlockSpec(memory_space=pltpu.SMEM),
-            pl.BlockSpec(memory_space=pltpu.VMEM),
-            pl.BlockSpec(memory_space=pltpu.HBM),
-            pl.BlockSpec(memory_space=pltpu.HBM),
-        ],
-        out_specs=pl.BlockSpec(memory_space=pltpu.VMEM),
-        out_shape=jax.ShapeDtypeStruct((groups, 2, count // groups), jnp.float32),
-        scratch_shapes=[
+    per, full = operands[0].shape
+    vmem = pl.BlockSpec(memory_space=pltpu.VMEM)
+    weights = pl.BlockSpec(memory_space=pltpu.HBM) if staged else vmem
+    scratch = [pltpu.VMEM((count, full), jnp.bfloat16)]
+    if staged:
+        scratch += [
             pltpu.VMEM((2, vocab, width), jnp.bfloat16),
             pltpu.SemaphoreType.DMA((3,)),
-        ],
+        ]
+    return pl.pallas_call(
+        kernel,
+        in_specs=[pl.BlockSpec(memory_space=pltpu.SMEM), weights, weights]
+        + [vmem] * len(operands),
+        out_specs=vmem,
+        out_shape=jax.ShapeDtypeStruct((groups, 2, per), jnp.float32),
+        scratch_shapes=scratch,
         cost_estimate=pl.CostEstimate(
             flops=4 * count * width * vocab,
             bytes_accessed=2 * width * (count + 2 * vocab),
             transcendentals=2 * count * vocab,
         ),
-        compiler_params=pltpu.CompilerParams(vmem_limit_bytes=KERNEL_VMEM),
-        name="shard_stats",
-    )(starts, rows, own, other)
+        compiler_params=pltpu.CompilerParams(
+            vmem_limit_bytes=KERNEL_VMEM if staged else LATE_VMEM
+        ),
+        name="early_stats" if staged else "late_stats",
+    )(scalars, own, other, *operands)
 
 
 def merged(lse):
@@ -229,7 +272,6 @@
 ):
     _, local_rows, width = hidden.shape
     vocab_rows = unembed.shape[0]
-    n_x = lax.axis_size("x")
     n_y = lax.axis_size("y")
     n_z = lax.axis_size(Z)
     column_rows = n_z * local_rows
@@ -244,8 +286,14 @@
     column = column.reshape(n_z, *chunk.shape)
     rows = column[:, : local_rows * full // LANES].reshape(column_rows, full)
 
+    up = [(i, (i + 1) % n_y) for i in range(n_y)]
+    down = [(i, (i - 1) % n_y) for i in range(n_y)]
+    below = lax.ppermute(rows, "y", up)
+    above = lax.ppermute(rows, "y", down)
     other_unembed = lax.ppermute(unembed, "c", [(0, 1), (1, 0)])
-    gathered = from_everyone(rows, "y").reshape(n_y * column_rows, full)
+    half = column_rows // 2
+    across_low = lax.ppermute(below[:half], "y", up)
+    across_high = lax.ppermute(above[half:], "y", down)
 
     side = rows[:, width : width + 3 * FIELDS].astype(jnp.float32).T
     side = side.reshape(FIELDS, 3, column_rows)
@@ -253,14 +301,24 @@
     valid_f = side[4:5]
     scores = side[5:6] * reward_unit
     moments = jnp.concatenate([valid_f, valid_f * scores, valid_f * scores * scores])
-    terms = [moments]
-    for d in range(1, n_x):
-        ring = [(i, (i + d) % n_x) for i in range(n_x)]
-        terms.append(lax.ppermute(moments, "x", ring))
-    adv_rows = group_advantages(sum(terms), valid_f, scores)
+    terms = from_everyone(moments, "x")
+    adv_rows = group_advantages(jnp.sum(terms, axis=0), valid_f, scores)
     z = lax.axis_index(Z)
-    shards = jnp.stack([(z * 2 + core) * n_y, (z * 2 + 1 - core) * n_y]) + y
-    stats = shard_stats(gathered, unembed, other_unembed, shards * vocab_rows, n_y)
+    scalars = jnp.stack(
+        [
+            ((z * 2 + core) * n_y + y) * vocab_rows,
+            ((z * 2 + 1 - core) * n_y + y) * vocab_rows,
+            y,
+        ]
+    )
+    stats = shard_stats(
+        early_kernel, scalars, unembed, other_unembed, [rows, above, below], 3,
+        2 * column_rows + FIRST, True,
+    )
+    stats = shard_stats(
+        late_kernel, scalars, unembed, other_unembed, [below, across_low, across_high, stats],
+        n_y, 2 * column_rows - FIRST, False,
+    )
     plane = lax.all_to_all(stats, "y", 0, 0, tiled=True)
     plane = jnp.concatenate([merged(plane[:, 0:1]), jnp.sum(plane[:, 1:2], axis=0)])
     back = from_everyone(plane, Z)
@@ -297,4 +355,6 @@
         P(PROMPT, "x"),
     )
     out_specs = (P("x", ROW), P("x", ROW), P(PROMPT, "x"), P())
-    return jax.shard_map(local, mesh=split, in_specs=in_specs, out_specs=out_specs, check_vma=False)
+    return jax.shard_map(
+        local, mesh=split, in_specs=in_specs, out_specs=out_specs, check_vma=False
+    )

time: 171 us -> 175 us (1.023)
  waiting for transfers between devices: 45.9 us -> 38.5 us
  starting transfers between devices: 63.3 us -> 70.4 us
  Pallas kernels: 11.6 us -> 16.9 us
    all_to_all x2, waiting for transfers between devices: 35.7 us -> 21.4 us  [from_everyone(): lax.all_to_all(jnp.broadcast_to(array[None], (devices, *array.shape)), ax...]
    ppermute x3 -> x4, waiting for transfers between devices: 0.01 us -> 6.75 us  [the longest x1 6.48 us: local(): below = lax.ppermute(rows, 'y', up)]
    all_to_all x1, starting transfers between devices: 16 us -> 21.5 us  [local(): lax.all_to_all(totals, PLANE, 0, 0, tiled=True)]
    pallas_call x1 -> x2, Pallas kernels: 8.69 us -> 13.9 us  [shard_stats(): pl.pallas_call(kernel, in_specs=[pl.BlockSpec(memory_space=pltpu.SMEM), w...]
    ppermute x3 -> x4, starting transfers between devices: 9.93 us -> 12.8 us  [the longest x1 4.3 us: local(): across_high = lax.ppermute(above[half:], 'y', down)]
    broadcast_in_dim x3 -> x2, local copies, waits for them, and re-layouts: 3.19 us -> 1.21 us  [from_everyone(): jnp.broadcast_to(array[None], (devices, *array.shape))]
  transfers between devices with their start and end apart: 8 -> 9, of which waited for: 4 -> 5; matrix products, arithmetic and copies ran while one was open for 3% -> 2% of each run, Pallas kernels for 6% -> 9%
where the time goes in v4:
time: 175 us; the launch traced here: 174 us
  starting transfers between devices  70.4 us (40%)
  waiting for transfers between devices  38.5 us (22%)
  blocking collectives  38 us (22%)
  Pallas kernels  16.9 us (10%)
  between operations  5.24 us (3%)
  local copies, waits for them, and re-layouts  4.68 us (3%)
    all_gather x2, blocking collectives, local(): column = lax.all_gather(lax.all_gather(chunk, 'zh', axis=0), 'zl', axis=0)  38 us
    all_to_all x1, starting transfers between devices, local(): lax.all_to_all(totals, PLANE, 0, 0, tiled=True)  21.5 us
    all_to_all x2, waiting for transfers between devices, from_everyone(): lax.all_to_all(jnp.broadcast_to(array[None], (devices, *array.shape)), ax...  21.4 us
    all_to_all x2, starting transfers between devices, from_everyone(): lax.all_to_all(jnp.broadcast_to(array[None], (devices, *array.shape)), ax...  16.8 us
    ppermute x1, starting transfers between devices, local(): other_unembed = lax.ppermute(unembed, 'c', [(0, 1), (1, 0)])  16 us
    pallas_call x2, Pallas kernels, shard_stats(): pl.pallas_call(kernel, in_specs=[pl.BlockSpec(memory_space=pltpu.SMEM), w...  13.9 us
    ppermute x1, waiting for transfers between devices, local(): below = lax.ppermute(rows, 'y', up)  6.48 us
    all_to_all x1, waiting for transfers between devices, local(): lax.all_to_all(totals, PLANE, 0, 0, tiled=True)  6.29 us
  transfers between devices with their start and end apart: 9, of which 5 were waited for; matrix products, arithmetic and copies ran while one was open for 2% of the time, Pallas kernels for 9%

profile of v4, /device:TPU:1, one launch (start us, length us, event | category | flops | bytes accessed | tf_op | source)
XLA Modules:
  0.0 174.0 jit_solution(3397618125187184748)
XLA Ops:
  0.6 16.0 %collective-permute-start = (bf16[594,3584]{1,0:T(8,128)(2,1)}, bf16[594,3584]{1,0:T(8,128)(2,1)}, u32[]{:S(2)}, u32[]{:S(2)}) collective-permute-start(bf16[594,3584]{1,0:T(8,128)(2,1)} %own_ref.3), channel_id=1, source_target_pairs={{0,16},{16,0},{1,17},{17,1},{2,18},{18,2},{3,19},{19,3},{4,20},{20... | collective-permute-start | bytes 12773384 | tf_op jit(solution)/shard_map/ppermute | solution.py:293
  18.6 2.2 %prep.1 = bf16[88,128]{1,0:T(8,128)(2,1)} custom-call(s32[1]{0:T(128)} %bitcast.2.y_ref, s32[1,3]{1,0:T(1,128)} %refs_0_.1, f32[1,3]{1,0:T(1,128)} %refs_1_.1, f32[1,3]{1,0:T(1,128)} %refs_2_.1, s32[1,3]{1,0:T(1,128)} %refs_3_.1, s32[1]{0:T(128)} %bitcast.33.refs_4_, s32[1]{0:T(128)} %bitcast.34.refs_5_, s32[1]{0:T(128)} %bitcast.35.refs_6_, ...), custom_call_target="tpu_custom_call" | custom-call | tf_op jit(solution)/shard_map/prep/pallas_call | solution.py:91
  20.8 30.6 %all-gather = bf16[1408,128]{1,0:T(8,128)(2,1)S(1)} all-gather(bf16[88,128]{1,0:T(8,128)(2,1)} %prep.1), channel_id=2, replica_groups=mesh['zh'=16,'zl'=2,'c'=2,'x'=4,'y'=4] {'zh'}, dimensions={0}, use_global_device_ids=true | all-gather | bytes 382976 | tf_op jit(solution)/shard_map/all_gather | solution.py:285
  51.4 7.4 %all-gather.1 = bf16[32,88,128]{2,1,0:T(8,128)(2,1)S(1)} all-gather(bf16[16,88,128]{2,1,0:T(8,128)(2,1)S(1)} %bitcast.40), channel_id=3, replica_groups=mesh['zh'=16,'zl'=2,'c'=2,'x'=4,'y'=4] {'zl'}, dimensions={0}, use_global_device_ids=true | all-gather | bytes 1081344 | tf_op jit(solution)/shard_map/all_gather | solution.py:285
  58.8 0.8 reshape.70.rows_ref
  59.6 3.2 %collective-permute-start.1 = (bf16[96,3712]{1,0:T(8,128)(2,1)S(1)}, bf16[96,3712]{1,0:T(8,128)(2,1)S(1)}, u32[]{:S(2)}, u32[]{:S(2)}) collective-permute-start(bf16[96,3712]{1,0:T(8,128)(2,1)S(1)} %reshape.70.rows_ref), channel_id=1, source_target_pairs={{0,1},{1,2},{2,3},{3,0},{4,5},{5,6},{6,7},{7,4},{8,9},{9,10},{10,1... | collective-permute-start | bytes 2138120 | tf_op jit(solution)/shard_map/ppermute | solution.py:291
  62.8 3.4 %collective-permute-start.3 = (bf16[96,3712]{1,0:T(8,128)(2,1)S(1)}, bf16[96,3712]{1,0:T(8,128)(2,1)S(1)}, u32[]{:S(2)}, u32[]{:S(2)}) collective-permute-start(bf16[96,3712]{1,0:T(8,128)(2,1)S(1)} %reshape.70.rows_ref), channel_id=1, source_target_pairs={{0,3},{1,0},{2,1},{3,2},{4,7},{5,4},{6,5},{7,6},{8,11},{9,8},{10,9... | collective-permute-start | bytes 2138120 | tf_op jit(solution)/shard_map/ppermute | solution.py:292
  66.3 6.5 %collective-permute-done.1.below_ref = bf16[96,3712]{1,0:T(8,128)(2,1)S(1)} collective-permute-done((bf16[96,3712]{1,0:T(8,128)(2,1)S(1)}, bf16[96,3712]{1,0:T(8,128)(2,1)S(1)}, u32[]{:S(2)}, u32[]{:S(2)}) %collective-permute-start.1) | collective-permute-done | bytes 712736 | tf_op jit(solution)/shard_map/ppermute | solution.py:291
  72.9 1.9 %collective-permute-start.2 = (bf16[48,3712]{1,0:T(8,128)(2,1)S(1)}, bf16[48,3712]{1,0:T(8,128)(2,1)S(1)}, u32[]{:S(2)}, u32[]{:S(2)}) collective-permute-start(bf16[48,3712]{1,0:T(8,128)(2,1)S(1)} %slice.70), channel_id=1, source_target_pairs={{0,1},{1,2},{2,3},{3,0},{4,5},{5,6},{6,7},{7,4},{8,9},{9,10},{10,1... | collective-permute-start | bytes 1069064 | tf_op jit(solution)/shard_map/ppermute | solution.py:295
  75.1 0.8 slice.71
  75.8 4.3 %collective-permute-start.4 = (bf16[48,3712]{1,0:T(8,128)(2,1)}, bf16[48,3712]{1,0:T(8,128)(2,1)S(1)}, u32[]{:S(2)}, u32[]{:S(2)}) collective-permute-start(bf16[48,3712]{1,0:T(8,128)(2,1)} %slice.71), channel_id=1, source_target_pairs={{0,3},{1,0},{2,1},{3,2},{4,7},{5,4},{6,5},{7,6},{8,11},{9,8},{10,9... | collective-permute-start | bytes 1069064 | tf_op jit(solution)/shard_map/ppermute | solution.py:296
  80.7 4.0 %all-to-all-start.2 = ((f32[4,3,96]{2,1,0:T(4,128)}), f32[4,3,96]{2,1,0:T(4,128)S(1)}, u32[]{:S(2)}, u32[]{:S(2)}) async-start(f32[4,3,96]{2,1,0:T(4,128)} %broadcast_in_dim.5), calls=%async_computation.2 | async-start | bytes 16384 | tf_op jit(solution)/shard_map/all_to_all | solution.py:31
  84.8 8.5 %early_stats.1.early_ref = f32[3,2,96]{2,1,0:T(2,128)S(1)} custom-call(s32[3]{0:T(128)S(1)} %pad_add_fusion.scalars_ref, bf16[594,3584]{1,0:T(8,128)(2,1)} %own_ref.3, bf16[594,3584]{1,0:T(8,128)(2,1)} %collective-permute-done.other_ref, bf16[96,3712]{1,0:T(8,128)(2,1)S(1)} %reshape.70.rows_ref, bf16[96,3712]{1,0:T(8,128)(2,1)S(1)} %collective-permute-done.3.above_ref, ...), custom_call_target="tpu_custom_call" | custom-call | flops 2179989504 | bytes 10350592 | tf_op jit(solution)/shard_map/early_stats/pallas_call | solution.py:238
  93.4 5.5 %late_stats.1 = f32[4,2,96]{2,1,0:T(2,128)} custom-call(s32[3]{0:T(128)S(1)} %pad_add_fusion.scalars_ref, bf16[594,3584]{1,0:T(8,128)(2,1)S(1)} %bitcast.37, bf16[594,3584]{1,0:T(8,128)(2,1)} %collective-permute-done.other_ref, bf16[96,3712]{1,0:T(8,128)(2,1)S(1)} %collective-permute-done.1.below_ref, bf16[48,3712]{1,0:T(8,128)(2,1)S(1)} %collective-permute-done.2.low_ref, ...), custom_call_target="tpu_custom_call" | custom-call | flops 1089994752 | bytes 9433088 | tf_op jit(solution)/shard_map/late_stats/pallas_call | solution.py:238
  98.8 3.2 %all-to-all-start = ((f32[4,2,96]{2,1,0:T(2,128)}), f32[4,2,96]{2,1,0:T(2,128)S(1)}, u32[]{:S(2)}, u32[]{:S(2)}) async-start(f32[4,2,96]{2,1,0:T(2,128)} %late_stats.1), calls=%async_computation | async-start | bytes 8192 | tf_op jit(solution)/shard_map/all_to_all | solution.py:322
  102.1 4.1 %all-to-all-done = f32[4,2,96]{2,1,0:T(2,128)S(1)} async-done(((f32[4,2,96]{2,1,0:T(2,128)}), f32[4,2,96]{2,1,0:T(2,128)S(1)}, u32[]{:S(2)}, u32[]{:S(2)}) %all-to-all-start) | async-done | bytes 3104 | tf_op jit(solution)/shard_map/all_to_all | solution.py:322
  106.3 0.6 broadcast_in_dim.4
  106.9 12.8 %all-to-all-start.1 = ((f32[32,2,96]{2,1,0:T(2,128)}), f32[32,2,96]{2,1,0:T(2,128)S(1)}, u32[]{:S(2)}, u32[]{:S(2)}) async-start(f32[32,2,96]{2,1,0:T(2,128)} %broadcast_in_dim.4), calls=%async_computation.1 | async-start | bytes 65536 | tf_op jit(solution)/shard_map/all_to_all | solution.py:31
  119.7 0.6 constant_dynamic-slice_fusion
  120.3 21.4 %all-to-all-done.1.back_ref = f32[32,2,96]{2,1,0:T(2,128)S(1)} async-done(((f32[32,2,96]{2,1,0:T(2,128)}), f32[32,2,96]{2,1,0:T(2,128)S(1)}, u32[]{:S(2)}, u32[]{:S(2)}) %all-to-all-start.1) | async-done | bytes 24608 | tf_op jit(solution)/shard_map/all_to_all | solution.py:31
  141.7 0.8 tail.1
  142.5 21.5 %all-to-all-start.3 = ((f32[32,1,128]{2,1,0:T(1,128)}), f32[32,1,128]{2,1,0:T(1,128)S(1)}, u32[]{:S(2)}, u32[]{:S(2)}) async-start(f32[32,1,128]{2,1,0:T(1,128)} %get-tuple-element.9), calls=%async_computation.3 | async-start | bytes 32768 | tf_op jit(solution)/shard_map/all_to_all | solution.py:327
  164.0 0.6 constant_dynamic-slice_fusion.1
  164.6 6.3 %all-to-all-done.3 = f32[32,1,128]{2,1,0:T(1,128)S(1)} async-done(((f32[32,1,128]{2,1,0:T(1,128)}), f32[32,1,128]{2,1,0:T(1,128)S(1)}, u32[]{:S(2)}, u32[]{:S(2)}) %all-to-all-start.3) | async-done | bytes 16416 | tf_op jit(solution)/shard_map/all_to_all | solution.py:327
  (29 shorter events, 1.9 us)
Async XLA Ops:
  0.6 84.2 %collective-permute-start = (bf16[594,3584]{1,0:T(8,128)(2,1)}, bf16[594,3584]{1,0:T(8,128)(2,1)}, u32[]{:S(2)}, u32[]{:S(2)}) collective-permute-start(bf16[594,3584]{1,0:T(8,128)(2,1)} %own_ref.3), channel_id=1, source_target_pairs={{0,16},{16,0},{1,17},{17,1},{2,18},{18,2},{3,19},{19,3},{4,20},{20... | collective-permute-start | bytes 12773384 | tf_op jit(solution)/shard_map/ppermute | solution.py:293
  59.6 13.2 %collective-permute-start.1 = (bf16[96,3712]{1,0:T(8,128)(2,1)S(1)}, bf16[96,3712]{1,0:T(8,128)(2,1)S(1)}, u32[]{:S(2)}, u32[]{:S(2)}) collective-permute-start(bf16[96,3712]{1,0:T(8,128)(2,1)S(1)} %reshape.70.rows_ref), channel_id=1, source_target_pairs={{0,1},{1,2},{2,3},{3,0},{4,5},{5,6},{6,7},{7,4},{8,9},{9,10},{10,1... | collective-permute-start | bytes 2138120 | tf_op jit(solution)/shard_map/ppermute | solution.py:291
  62.8 12.2 %collective-permute-start.3 = (bf16[96,3712]{1,0:T(8,128)(2,1)S(1)}, bf16[96,3712]{1,0:T(8,128)(2,1)S(1)}, u32[]{:S(2)}, u32[]{:S(2)}) collective-permute-start(bf16[96,3712]{1,0:T(8,128)(2,1)S(1)} %reshape.70.rows_ref), channel_id=1, source_target_pairs={{0,3},{1,0},{2,1},{3,2},{4,7},{5,4},{6,5},{7,6},{8,11},{9,8},{10,9... | collective-permute-start | bytes 2138120 | tf_op jit(solution)/shard_map/ppermute | solution.py:292
  72.9 20.5 %collective-permute-start.2 = (bf16[48,3712]{1,0:T(8,128)(2,1)S(1)}, bf16[48,3712]{1,0:T(8,128)(2,1)S(1)}, u32[]{:S(2)}, u32[]{:S(2)}) collective-permute-start(bf16[48,3712]{1,0:T(8,128)(2,1)S(1)} %slice.70), channel_id=1, source_target_pairs={{0,1},{1,2},{2,3},{3,0},{4,5},{5,6},{6,7},{7,4},{8,9},{9,10},{10,1... | collective-permute-start | bytes 1069064 | tf_op jit(solution)/shard_map/ppermute | solution.py:295
  75.8 17.5 %collective-permute-start.4 = (bf16[48,3712]{1,0:T(8,128)(2,1)}, bf16[48,3712]{1,0:T(8,128)(2,1)S(1)}, u32[]{:S(2)}, u32[]{:S(2)}) collective-permute-start(bf16[48,3712]{1,0:T(8,128)(2,1)} %slice.71), channel_id=1, source_target_pairs={{0,3},{1,0},{2,1},{3,2},{4,7},{5,4},{6,5},{7,6},{8,11},{9,8},{10,9... | collective-permute-start | bytes 1069064 | tf_op jit(solution)/shard_map/ppermute | solution.py:296
  80.7 18.1 %all-to-all-start.2 = ((f32[4,3,96]{2,1,0:T(4,128)}), f32[4,3,96]{2,1,0:T(4,128)S(1)}, u32[]{:S(2)}, u32[]{:S(2)}) async-start(f32[4,3,96]{2,1,0:T(4,128)} %broadcast_in_dim.5), calls=%async_computation.2 | async-start | bytes 16384 | tf_op jit(solution)/shard_map/all_to_all | solution.py:31
  84.8 8.6 %slice-start = ((s8[4300800]{0:T(1024)(128)(4,1)}), s8[4194304]{0:T(1024)(128)(4,1)S(1)}, s32[]{:S(2)}) async-start(s8[4300800]{0:T(1024)(128)(4,1)} %bitcast.36), calls=%async_computation.4 | async-start | bytes 8388608
  84.8 8.5 %slice-start.1 = ((s8[4300800]{0:T(1024)(128)(4,1)}), s8[106496]{0:T(1024)(128)(4,1)S(1)}, s32[]{:S(2)}) async-start(s8[4300800]{0:T(1024)(128)(4,1)} %bitcast.36), calls=%async_computation.5 | async-start | bytes 212992
  98.8 7.4 %all-to-all-start = ((f32[4,2,96]{2,1,0:T(2,128)}), f32[4,2,96]{2,1,0:T(2,128)S(1)}, u32[]{:S(2)}, u32[]{:S(2)}) async-start(f32[4,2,96]{2,1,0:T(2,128)} %late_stats.1), calls=%async_computation | async-start | bytes 8192 | tf_op jit(solution)/shard_map/all_to_all | solution.py:322
  106.9 34.8 %all-to-all-start.1 = ((f32[32,2,96]{2,1,0:T(2,128)}), f32[32,2,96]{2,1,0:T(2,128)S(1)}, u32[]{:S(2)}, u32[]{:S(2)}) async-start(f32[32,2,96]{2,1,0:T(2,128)} %broadcast_in_dim.4), calls=%async_computation.1 | async-start | bytes 65536 | tf_op jit(solution)/shard_map/all_to_all | solution.py:31
  142.5 28.4 %all-to-all-start.3 = ((f32[32,1,128]{2,1,0:T(1,128)}), f32[32,1,128]{2,1,0:T(1,128)S(1)}, u32[]{:S(2)}, u32[]{:S(2)}) async-start(f32[32,1,128]{2,1,0:T(1,128)} %get-tuple-element.9), calls=%async_computation.3 | async-start | bytes 32768 | tf_op jit(solution)/shard_map/all_to_all | solution.py:327

commit v5 on v4

--- a/solution.py
+++ b/solution.py
@@ -34,14 +34,15 @@
 
 
 def prep_kernel(y_ref, *refs):
-    smalls, hidden_ref, out_ref, tall_ref = refs[:7], refs[7], refs[8], refs[9]
-    landed, sems = refs[10:17], refs[17]
+    smalls, hidden_src, out_ref, tall_ref, hidden_ref = refs[:7], *refs[7:11]
+    landed, sems = refs[11:18], refs[18]
     copies = [
         pltpu.make_async_copy(src, dst, sems.at[i])
-        for i, (src, dst) in enumerate(zip(smalls, landed))
+        for i, (src, dst) in enumerate(zip((*smalls, hidden_src), (*landed, hidden_ref)))
     ]
     for copy in copies:
         copy.start()
+    tall_ref[...] = jnp.zeros(tall_ref.shape, jnp.float32)
     for copy in copies:
         copy.wait()
     ids_ref, old_ref, ref_ref, mask_ref, len_ref, valid_ref, reward_ref = landed
@@ -74,7 +75,6 @@
     second = rest.astype(jnp.bfloat16).astype(jnp.float32)
     piece = lane - 3 * field
     side = jnp.where(piece == 0, first, jnp.where(piece == 1, second, rest - second))
-    tall_ref[...] = jnp.zeros(tall_ref.shape, jnp.float32)
     for r in range(local_rows):
         at = r * (blocks + 1)
         for j in range(blocks):
@@ -91,14 +91,14 @@
     return pl.pallas_call(
         prep_kernel,
         in_specs=[pl.BlockSpec(memory_space=pltpu.SMEM)]
-        + [pl.BlockSpec(memory_space=pltpu.HBM)] * len(smalls)
-        + [vmem],
+        + [pl.BlockSpec(memory_space=pltpu.HBM)] * (len(smalls) + 1),
         out_specs=vmem,
         out_shape=jax.ShapeDtypeStruct((tall, LANES), jnp.bfloat16),
         scratch_shapes=[
             pltpu.VMEM((tall, LANES), jnp.float32),
+            pltpu.VMEM(hidden.shape, hidden.dtype),
             *(pltpu.SMEM(small.shape, small.dtype) for small in smalls),
-            pltpu.SemaphoreType.DMA((len(smalls),)),
+            pltpu.SemaphoreType.DMA((len(smalls) + 1,)),
         ],
         compiler_params=pltpu.CompilerParams(vmem_limit_bytes=FULL_VMEM),
         name="prep",

time: 175 us -> 174 us (level)
  no operation moved by 1% of the time
where the time goes in v5:
time: 174 us; the launch traced here: 173 us
  starting transfers between devices  70.4 us (40%)
  waiting for transfers between devices  38.5 us (22%)
  blocking collectives  38 us (22%)
  Pallas kernels  16.2 us (9%)
  between operations  5.24 us (3%)
  local copies, waits for them, and re-layouts  4.68 us (3%)
    all_gather x2, blocking collectives, local(): column = lax.all_gather(lax.all_gather(chunk, 'zh', axis=0), 'zl', axis=0)  38 us
    all_to_all x1, starting transfers between devices, local(): lax.all_to_all(totals, PLANE, 0, 0, tiled=True)  21.5 us
    all_to_all x2, waiting for transfers between devices, from_everyone(): lax.all_to_all(jnp.broadcast_to(array[None], (devices, *array.shape)), ax...  21.4 us
    all_to_all x2, starting transfers between devices, from_everyone(): lax.all_to_all(jnp.broadcast_to(array[None], (devices, *array.shape)), ax...  16.8 us
    ppermute x1, starting transfers between devices, local(): other_unembed = lax.ppermute(unembed, 'c', [(0, 1), (1, 0)])  16 us
    pallas_call x2, Pallas kernels, shard_stats(): pl.pallas_call(kernel, in_specs=[pl.BlockSpec(memory_space=pltpu.SMEM), w...  13.9 us
    ppermute x1, waiting for transfers between devices, local(): below = lax.ppermute(rows, 'y', up)  6.48 us
    all_to_all x1, waiting for transfers between devices, local(): lax.all_to_all(totals, PLANE, 0, 0, tiled=True)  6.29 us
  transfers between devices with their start and end apart: 9, of which 5 were waited for; matrix products, arithmetic and copies ran while one was open for 2% of the time, Pallas kernels for 9%

profile of v5, /device:TPU:1, one launch (start us, length us, event | category | flops | bytes accessed | tf_op | source)
XLA Modules:
  0.0 173.3 jit_solution(7464389260644526651)
XLA Ops:
  0.6 16.0 %collective-permute-start = (bf16[594,3584]{1,0:T(8,128)(2,1)}, bf16[594,3584]{1,0:T(8,128)(2,1)}, u32[]{:S(2)}, u32[]{:S(2)}) collective-permute-start(bf16[594,3584]{1,0:T(8,128)(2,1)} %own_ref.3), channel_id=1, source_target_pairs={{0,16},{16,0},{1,17},{17,1},{2,18},{18,2},{3,19},{19,3},{4,20},{20... | collective-permute-start | bytes 12773384 | tf_op jit(solution)/shard_map/ppermute | solution.py:293
  18.6 1.5 prep.1
  20.1 30.6 %all-gather = bf16[1408,128]{1,0:T(8,128)(2,1)S(1)} all-gather(bf16[88,128]{1,0:T(8,128)(2,1)} %prep.1), channel_id=2, replica_groups=mesh['zh'=16,'zl'=2,'c'=2,'x'=4,'y'=4] {'zh'}, dimensions={0}, use_global_device_ids=true | all-gather | bytes 382976 | tf_op jit(solution)/shard_map/all_gather | solution.py:285
  50.7 7.4 %all-gather.1 = bf16[32,88,128]{2,1,0:T(8,128)(2,1)S(1)} all-gather(bf16[16,88,128]{2,1,0:T(8,128)(2,1)S(1)} %bitcast.40), channel_id=3, replica_groups=mesh['zh'=16,'zl'=2,'c'=2,'x'=4,'y'=4] {'zl'}, dimensions={0}, use_global_device_ids=true | all-gather | bytes 1081344 | tf_op jit(solution)/shard_map/all_gather | solution.py:285
  58.1 0.8 reshape.70.rows_ref
  58.9 3.2 %collective-permute-start.1 = (bf16[96,3712]{1,0:T(8,128)(2,1)S(1)}, bf16[96,3712]{1,0:T(8,128)(2,1)S(1)}, u32[]{:S(2)}, u32[]{:S(2)}) collective-permute-start(bf16[96,3712]{1,0:T(8,128)(2,1)S(1)} %reshape.70.rows_ref), channel_id=1, source_target_pairs={{0,1},{1,2},{2,3},{3,0},{4,5},{5,6},{6,7},{7,4},{8,9},{9,10},{10,1... | collective-permute-start | bytes 2138120 | tf_op jit(solution)/shard_map/ppermute | solution.py:291
  62.1 3.4 %collective-permute-start.3 = (bf16[96,3712]{1,0:T(8,128)(2,1)S(1)}, bf16[96,3712]{1,0:T(8,128)(2,1)S(1)}, u32[]{:S(2)}, u32[]{:S(2)}) collective-permute-start(bf16[96,3712]{1,0:T(8,128)(2,1)S(1)} %reshape.70.rows_ref), channel_id=1, source_target_pairs={{0,3},{1,0},{2,1},{3,2},{4,7},{5,4},{6,5},{7,6},{8,11},{9,8},{10,9... | collective-permute-start | bytes 2138120 | tf_op jit(solution)/shard_map/ppermute | solution.py:292
  65.6 6.5 %collective-permute-done.1.below_ref = bf16[96,3712]{1,0:T(8,128)(2,1)S(1)} collective-permute-done((bf16[96,3712]{1,0:T(8,128)(2,1)S(1)}, bf16[96,3712]{1,0:T(8,128)(2,1)S(1)}, u32[]{:S(2)}, u32[]{:S(2)}) %collective-permute-start.1) | collective-permute-done | bytes 712736 | tf_op jit(solution)/shard_map/ppermute | solution.py:291
  72.2 1.9 %collective-permute-start.2 = (bf16[48,3712]{1,0:T(8,128)(2,1)S(1)}, bf16[48,3712]{1,0:T(8,128)(2,1)S(1)}, u32[]{:S(2)}, u32[]{:S(2)}) collective-permute-start(bf16[48,3712]{1,0:T(8,128)(2,1)S(1)} %slice.70), channel_id=1, source_target_pairs={{0,1},{1,2},{2,3},{3,0},{4,5},{5,6},{6,7},{7,4},{8,9},{9,10},{10,1... | collective-permute-start | bytes 1069064 | tf_op jit(solution)/shard_map/ppermute | solution.py:295
  74.4 0.8 slice.71
  75.1 4.3 %collective-permute-start.4 = (bf16[48,3712]{1,0:T(8,128)(2,1)}, bf16[48,3712]{1,0:T(8,128)(2,1)S(1)}, u32[]{:S(2)}, u32[]{:S(2)}) collective-permute-start(bf16[48,3712]{1,0:T(8,128)(2,1)} %slice.71), channel_id=1, source_target_pairs={{0,3},{1,0},{2,1},{3,2},{4,7},{5,4},{6,5},{7,6},{8,11},{9,8},{10,9... | collective-permute-start | bytes 1069064 | tf_op jit(solution)/shard_map/ppermute | solution.py:296
  80.0 4.0 %all-to-all-start.2 = ((f32[4,3,96]{2,1,0:T(4,128)}), f32[4,3,96]{2,1,0:T(4,128)S(1)}, u32[]{:S(2)}, u32[]{:S(2)}) async-start(f32[4,3,96]{2,1,0:T(4,128)} %broadcast_in_dim.5), calls=%async_computation.2 | async-start | bytes 16384 | tf_op jit(solution)/shard_map/all_to_all | solution.py:31
  84.1 8.5 %early_stats.1.early_ref = f32[3,2,96]{2,1,0:T(2,128)S(1)} custom-call(s32[3]{0:T(128)S(1)} %pad_add_fusion.scalars_ref, bf16[594,3584]{1,0:T(8,128)(2,1)} %own_ref.3, bf16[594,3584]{1,0:T(8,128)(2,1)} %collective-permute-done.other_ref, bf16[96,3712]{1,0:T(8,128)(2,1)S(1)} %reshape.70.rows_ref, bf16[96,3712]{1,0:T(8,128)(2,1)S(1)} %collective-permute-done.3.above_ref, ...), custom_call_target="tpu_custom_call" | custom-call | flops 2179989504 | bytes 10350592 | tf_op jit(solution)/shard_map/early_stats/pallas_call | solution.py:238
  92.7 5.5 %late_stats.1 = f32[4,2,96]{2,1,0:T(2,128)} custom-call(s32[3]{0:T(128)S(1)} %pad_add_fusion.scalars_ref, bf16[594,3584]{1,0:T(8,128)(2,1)S(1)} %bitcast.37, bf16[594,3584]{1,0:T(8,128)(2,1)} %collective-permute-done.other_ref, bf16[96,3712]{1,0:T(8,128)(2,1)S(1)} %collective-permute-done.1.below_ref, bf16[48,3712]{1,0:T(8,128)(2,1)S(1)} %collective-permute-done.2.low_ref, ...), custom_call_target="tpu_custom_call" | custom-call | flops 1089994752 | bytes 9433088 | tf_op jit(solution)/shard_map/late_stats/pallas_call | solution.py:238
  98.1 3.2 %all-to-all-start = ((f32[4,2,96]{2,1,0:T(2,128)}), f32[4,2,96]{2,1,0:T(2,128)S(1)}, u32[]{:S(2)}, u32[]{:S(2)}) async-start(f32[4,2,96]{2,1,0:T(2,128)} %late_stats.1), calls=%async_computation | async-start | bytes 8192 | tf_op jit(solution)/shard_map/all_to_all | solution.py:322
  101.4 4.1 %all-to-all-done = f32[4,2,96]{2,1,0:T(2,128)S(1)} async-done(((f32[4,2,96]{2,1,0:T(2,128)}), f32[4,2,96]{2,1,0:T(2,128)S(1)}, u32[]{:S(2)}, u32[]{:S(2)}) %all-to-all-start) | async-done | bytes 3104 | tf_op jit(solution)/shard_map/all_to_all | solution.py:322
  105.6 0.6 broadcast_in_dim.4
  106.2 12.8 %all-to-all-start.1 = ((f32[32,2,96]{2,1,0:T(2,128)}), f32[32,2,96]{2,1,0:T(2,128)S(1)}, u32[]{:S(2)}, u32[]{:S(2)}) async-start(f32[32,2,96]{2,1,0:T(2,128)} %broadcast_in_dim.4), calls=%async_computation.1 | async-start | bytes 65536 | tf_op jit(solution)/shard_map/all_to_all | solution.py:31
  119.0 0.6 constant_dynamic-slice_fusion
  119.6 21.4 %all-to-all-done.1.back_ref = f32[32,2,96]{2,1,0:T(2,128)S(1)} async-done(((f32[32,2,96]{2,1,0:T(2,128)}), f32[32,2,96]{2,1,0:T(2,128)S(1)}, u32[]{:S(2)}, u32[]{:S(2)}) %all-to-all-start.1) | async-done | bytes 24608 | tf_op jit(solution)/shard_map/all_to_all | solution.py:31
  141.0 0.8 tail.1
  141.8 21.5 %all-to-all-start.3 = ((f32[32,1,128]{2,1,0:T(1,128)}), f32[32,1,128]{2,1,0:T(1,128)S(1)}, u32[]{:S(2)}, u32[]{:S(2)}) async-start(f32[32,1,128]{2,1,0:T(1,128)} %get-tuple-element.9), calls=%async_computation.3 | async-start | bytes 32768 | tf_op jit(solution)/shard_map/all_to_all | solution.py:327
  163.3 0.6 constant_dynamic-slice_fusion.1
  163.9 6.3 %all-to-all-done.3 = f32[32,1,128]{2,1,0:T(1,128)S(1)} async-done(((f32[32,1,128]{2,1,0:T(1,128)}), f32[32,1,128]{2,1,0:T(1,128)S(1)}, u32[]{:S(2)}, u32[]{:S(2)}) %all-to-all-start.3) | async-done | bytes 16416 | tf_op jit(solution)/shard_map/all_to_all | solution.py:327
  (29 shorter events, 1.9 us)
Async XLA Ops:
  0.6 83.5 %collective-permute-start = (bf16[594,3584]{1,0:T(8,128)(2,1)}, bf16[594,3584]{1,0:T(8,128)(2,1)}, u32[]{:S(2)}, u32[]{:S(2)}) collective-permute-start(bf16[594,3584]{1,0:T(8,128)(2,1)} %own_ref.3), channel_id=1, source_target_pairs={{0,16},{16,0},{1,17},{17,1},{2,18},{18,2},{3,19},{19,3},{4,20},{20... | collective-permute-start | bytes 12773384 | tf_op jit(solution)/shard_map/ppermute | solution.py:293
  58.9 13.2 %collective-permute-start.1 = (bf16[96,3712]{1,0:T(8,128)(2,1)S(1)}, bf16[96,3712]{1,0:T(8,128)(2,1)S(1)}, u32[]{:S(2)}, u32[]{:S(2)}) collective-permute-start(bf16[96,3712]{1,0:T(8,128)(2,1)S(1)} %reshape.70.rows_ref), channel_id=1, source_target_pairs={{0,1},{1,2},{2,3},{3,0},{4,5},{5,6},{6,7},{7,4},{8,9},{9,10},{10,1... | collective-permute-start | bytes 2138120 | tf_op jit(solution)/shard_map/ppermute | solution.py:291
  62.1 12.2 %collective-permute-start.3 = (bf16[96,3712]{1,0:T(8,128)(2,1)S(1)}, bf16[96,3712]{1,0:T(8,128)(2,1)S(1)}, u32[]{:S(2)}, u32[]{:S(2)}) collective-permute-start(bf16[96,3712]{1,0:T(8,128)(2,1)S(1)} %reshape.70.rows_ref), channel_id=1, source_target_pairs={{0,3},{1,0},{2,1},{3,2},{4,7},{5,4},{6,5},{7,6},{8,11},{9,8},{10,9... | collective-permute-start | bytes 2138120 | tf_op jit(solution)/shard_map/ppermute | solution.py:292
  72.2 20.5 %collective-permute-start.2 = (bf16[48,3712]{1,0:T(8,128)(2,1)S(1)}, bf16[48,3712]{1,0:T(8,128)(2,1)S(1)}, u32[]{:S(2)}, u32[]{:S(2)}) collective-permute-start(bf16[48,3712]{1,0:T(8,128)(2,1)S(1)} %slice.70), channel_id=1, source_target_pairs={{0,1},{1,2},{2,3},{3,0},{4,5},{5,6},{6,7},{7,4},{8,9},{9,10},{10,1... | collective-permute-start | bytes 1069064 | tf_op jit(solution)/shard_map/ppermute | solution.py:295
  75.1 17.5 %collective-permute-start.4 = (bf16[48,3712]{1,0:T(8,128)(2,1)}, bf16[48,3712]{1,0:T(8,128)(2,1)S(1)}, u32[]{:S(2)}, u32[]{:S(2)}) collective-permute-start(bf16[48,3712]{1,0:T(8,128)(2,1)} %slice.71), channel_id=1, source_target_pairs={{0,3},{1,0},{2,1},{3,2},{4,7},{5,4},{6,5},{7,6},{8,11},{9,8},{10,9... | collective-permute-start | bytes 1069064 | tf_op jit(solution)/shard_map/ppermute | solution.py:296
  80.0 18.1 %all-to-all-start.2 = ((f32[4,3,96]{2,1,0:T(4,128)}), f32[4,3,96]{2,1,0:T(4,128)S(1)}, u32[]{:S(2)}, u32[]{:S(2)}) async-start(f32[4,3,96]{2,1,0:T(4,128)} %broadcast_in_dim.5), calls=%async_computation.2 | async-start | bytes 16384 | tf_op jit(solution)/shard_map/all_to_all | solution.py:31
  84.1 8.6 %slice-start = ((s8[4300800]{0:T(1024)(128)(4,1)}), s8[4194304]{0:T(1024)(128)(4,1)S(1)}, s32[]{:S(2)}) async-start(s8[4300800]{0:T(1024)(128)(4,1)} %bitcast.36), calls=%async_computation.4 | async-start | bytes 8388608
  84.1 8.5 %slice-start.1 = ((s8[4300800]{0:T(1024)(128)(4,1)}), s8[106496]{0:T(1024)(128)(4,1)S(1)}, s32[]{:S(2)}) async-start(s8[4300800]{0:T(1024)(128)(4,1)} %bitcast.36), calls=%async_computation.5 | async-start | bytes 212992
  98.1 7.4 %all-to-all-start = ((f32[4,2,96]{2,1,0:T(2,128)}), f32[4,2,96]{2,1,0:T(2,128)S(1)}, u32[]{:S(2)}, u32[]{:S(2)}) async-start(f32[4,2,96]{2,1,0:T(2,128)} %late_stats.1), calls=%async_computation | async-start | bytes 8192 | tf_op jit(solution)/shard_map/all_to_all | solution.py:322
  106.2 34.8 %all-to-all-start.1 = ((f32[32,2,96]{2,1,0:T(2,128)}), f32[32,2,96]{2,1,0:T(2,128)S(1)}, u32[]{:S(2)}, u32[]{:S(2)}) async-start(f32[32,2,96]{2,1,0:T(2,128)} %broadcast_in_dim.4), calls=%async_computation.1 | async-start | bytes 65536 | tf_op jit(solution)/shard_map/all_to_all | solution.py:31
  141.8 28.4 %all-to-all-start.3 = ((f32[32,1,128]{2,1,0:T(1,128)}), f32[32,1,128]{2,1,0:T(1,128)S(1)}, u32[]{:S(2)}, u32[]{:S(2)}) async-start(f32[32,1,128]{2,1,0:T(1,128)} %get-tuple-element.9), calls=%async_computation.3 | async-start | bytes 32768 | tf_op jit(solution)/shard_map/all_to_all | solution.py:327
